TPU v7x, 32 devices: a whole 2x2x4 slice. The times are simulated.
32 devices in a mesh: depth: 16 (over z, y, x), chan: 2 (over core).
Axes of the slice: x: 2, y: 2, z: 4, core: 2. Of those that a mesh axis runs over, the one named last changes fastest.
Arguments:
- feats: bfloat16 [32, 32, 8, 128], P('chan', 'depth'), may hold values from -6 to 6
- weight_one: bfloat16 [32, 32, 27], replicated, may hold values from -0.21875 to 0.21875
- weight_two: bfloat16 [64, 32, 27], replicated, may hold values from -0.21875 to 0.21875
- cotangent: bfloat16 [64, 16, 4, 64], P('chan', 'depth'), may hold values from -6 to 6
Outputs:
- grad_feats: bfloat16 [32, 32, 8, 128], P('chan', 'depth')
- grad_weight_one: float32 [32, 32, 27], P(None, 'chan')
- grad_weight_two: float32 [64, 32, 27], P(None, 'chan')
All inputs are finite; a program needn't handle non-finite values.
Results may differ from a plain program's by a relative error of at most 0.013.
Values may be sent and summed in bfloat16 or wider, within the bound.
A program may use at most 128 MiB of HBM per device.

v0:
```python
import jax
import jax.numpy as jnp
from jax import lax
from jax.sharding import PartitionSpec as P

OFFSETS = [
    (first, second, third) for first in range(3) for second in range(3) for third in range(3)
]


def padded_2(block, sides, width):
    for axis, dim in sides:
        count = lax.axis_size(axis)
        forward = [(i, i + 1) for i in range(count - 1)]
        backward = [(target, source) for source, target in forward]
        low = lax.ppermute(
            lax.slice_in_dim(block, block.shape[dim] - width, None, axis=dim), axis, forward
        )
        high = lax.ppermute(lax.slice_in_dim(block, 0, width, axis=dim), axis, backward)
        block = jnp.concatenate([low, block, high], axis=dim)
    return block


def pad_plane(haloed):
    return jnp.pad(haloed, ((0, 0), (0, 0), (1, 1), (1, 1)))


def cut_edges(haloed, lower_keep, upper_keep):
    count = haloed.shape[1]
    position = lax.iota(jnp.int32, count)
    keep = jnp.where(position == 0, lower_keep, jnp.where(position == count - 1, upper_keep, True))
    return jnp.where(keep[None, :, None, None], haloed, jnp.zeros((), haloed.dtype))


def patch_rows(haloed):
    chans = haloed.shape[0]
    planes = haloed.shape[1] - 2
    height = haloed.shape[2]
    across = haloed.shape[3]
    padded = pad_plane(haloed)
    windows = [
        padded[:, first : first + planes, second : second + height, third : third + across]
        for first, second, third in OFFSETS
    ]
    return jnp.stack(windows, 0).reshape(27 * chans, planes * height * across)


def flat_weight(own):
    return jnp.transpose(own, (0, 2, 1)).reshape(own.shape[0], -1)


def flat_transposed(own):
    return jnp.transpose(own, (2, 1, 0)).reshape(-1, own.shape[0])


def weight_layout(weight_sum, chans):
    return jnp.transpose(weight_sum.reshape(weight_sum.shape[0], 27, chans), (0, 2, 1))


def slope(pre):
    sig = jax.nn.sigmoid(pre)
    return sig * (1.0 + pre * (1.0 - sig))


def grad_fold(transposed, patches, piece):
    count = piece.shape[0]
    padded = pad_plane(piece).reshape(count, -1)
    image_sum = jnp.dot(transposed, padded, preferred_element_type=jnp.float32)
    inner = piece[:, 1:-1].reshape(count, -1)
    rows_part = lax.dot_general(
        inner, patches, (((1,), (1,)), ((), ())), preferred_element_type=jnp.float32
    )
    return (image_sum, rows_part)


def shift_sum(image_sum, chans, planes, height, across):
    shaped = image_sum.reshape(27, chans, planes + 2, height + 2, across + 2)
    total = jnp.zeros((chans, planes, height, across), jnp.float32)
    for index, (first, second, third) in enumerate(OFFSETS):
        total = (
            total
            + shaped[
                index,
                :,
                2 - first : 2 - first + planes,
                2 - second : 2 - second + height,
                2 - third : 2 - third + across,
            ]
        )
    return total


def shards(feats, weight_one, weight_two, cotangent):
    groups = lax.axis_size("chan")
    member = lax.axis_index("chan")
    slabs = lax.axis_size("depth")
    place = lax.axis_index("depth")
    lower_keep = place % slabs != 0
    upper_keep = (place + 1) % slabs != 0
    in_chans, planes, height, across = feats.shape
    mid_chans = weight_one.shape[0] // groups
    out_chans = weight_two.shape[0] // groups
    feats_halo = cut_edges(padded_2(feats, (("depth", 1),), 1), lower_keep, upper_keep)
    patches_one = patch_rows(feats_halo)
    own_one = lax.dynamic_slice_in_dim(weight_one, member * in_chans, in_chans, 1)
    partial_one = jnp.dot(flat_weight(own_one), patches_one, preferred_element_type=jnp.float32)
    pre_one = lax.psum_scatter(
        partial_one.astype(jnp.bfloat16), "chan", scatter_dimension=0, tiled=True
    ).astype(jnp.float32)
    act_one = jax.nn.silu(pre_one).astype(jnp.bfloat16).reshape(mid_chans, planes, height, across)
    pooled = (
        act_one.astype(jnp.float32)
        .reshape(mid_chans, planes // 2, 2, height // 2, 2, across // 2, 2)
        .mean(axis=(2, 4, 6))
        .astype(jnp.bfloat16)
    )
    pooled_halo = cut_edges(padded_2(pooled, (("depth", 1),), 1), lower_keep, upper_keep)
    patches_two = patch_rows(pooled_halo)
    own_two = lax.dynamic_slice_in_dim(weight_two, member * mid_chans, mid_chans, 1)
    partial_two = jnp.dot(flat_weight(own_two), patches_two, preferred_element_type=jnp.float32)
    pre_two = lax.psum_scatter(
        partial_two.astype(jnp.bfloat16), "chan", scatter_dimension=0, tiled=True
    ).astype(jnp.float32)
    grad_two = (cotangent.astype(jnp.float32).reshape(out_chans, -1) * slope(pre_two)).astype(
        jnp.bfloat16
    )
    grad_two = grad_two.reshape(out_chans, planes // 2, height // 2, across // 2)
    grad_two_halo = cut_edges(padded_2(grad_two, (("depth", 1),), 1), lower_keep, upper_keep)
    image_two, wsum_two = grad_fold(
        flat_transposed(own_two),
        patches_two,
        lax.all_gather(grad_two_halo, "chan", axis=0, tiled=True),
    )
    grad_weight_two = weight_layout(wsum_two, mid_chans)
    grad_weight_two = lax.psum(grad_weight_two, "depth")
    back_pooled = shift_sum(image_two, mid_chans, planes // 2, height // 2, across // 2)
    spread = (
        jnp.broadcast_to(
            back_pooled[:, :, None, :, None, :, None],
            (mid_chans, planes // 2, 2, height // 2, 2, across // 2, 2),
        ).reshape(mid_chans, -1)
        * 0.125
    )
    grad_one = (
        (spread * slope(pre_one)).astype(jnp.bfloat16).reshape(mid_chans, planes, height, across)
    )
    grad_one_halo = cut_edges(padded_2(grad_one, (("depth", 1),), 1), lower_keep, upper_keep)
    image_one, wsum_one = grad_fold(
        flat_transposed(own_one),
        patches_one,
        lax.all_gather(grad_one_halo, "chan", axis=0, tiled=True),
    )
    grad_weight_one = weight_layout(wsum_one, in_chans)
    grad_weight_one = lax.psum(grad_weight_one, "depth")
    grad_feats = shift_sum(image_one, in_chans, planes, height, across).astype(jnp.bfloat16)
    return (grad_feats, grad_weight_one, grad_weight_two)


def solution(mesh):
    return jax.shard_map(
        shards,
        mesh=mesh,
        in_specs=(P("chan", "depth", None, None), P(), P(), P("chan", "depth", None, None)),
        out_specs=(P("chan", "depth", None, None), P(None, "chan", None), P(None, "chan", None)),
        check_vma=False,
    )
```

profile of v0, /device:TPU:0, one launch (start us, length us, event | category | flops | bytes accessed | tf_op | source)
XLA Modules:
  0.0 237.0 jit_solution(2081670601970649039)
XLA Ops:
  7.2 0.9 copy.1996
  8.2 4.9 %collective-permute-start = (bf16[16,1,8,128]{3,0,2,1:T(8,128)(2,1)S(1)}, bf16[16,1,8,128]{3,0,2,1:T(8,128)(2,1)S(1)}, u32[]{:S(2)}, u32[]{:S(2)}) collective-permute-start(bf16[16,1,8,128]{3,0,2,1:T(8,128)(2,1)S(1)} %get-tuple-element.146), channel_id=1, source_target_pairs={{0,2},{2,4},{4,6},{6,8},{8,10},{10,12},{12,14},{14,16},{16,18},{18... | collective-permute-start | bytes 98312 | tf_op jit(solution)/shard_map/ppermute | solution.py:16
  13.0 1.3 collective-permute-start.1
  14.4 1.1 constant_dynamic-slice_fusion.1
  15.6 3.2 %collective-permute-done.1 = bf16[16,1,8,128]{3,0,2,1:T(8,128)(2,1)S(1)} collective-permute-done((bf16[16,1,8,128]{3,0,2,1:T(8,128)(2,1)S(1)}, bf16[16,1,8,128]{3,0,2,1:T(8,128)(2,1)S(1)}, u32[]{:S(2)}, u32[]{:S(2)}) %collective-permute-start.1) | collective-permute-done | bytes 32800 | tf_op jit(solution)/shard_map/ppermute | solution.py:19
  21.0 0.8 copy.2027
  21.8 0.8 copy.2028
  22.6 0.8 copy.2029
  25.6 0.8 copy.2034
  26.3 0.8 copy.2035
  27.8 0.8 copy.2037
  28.6 0.8 copy.2038
  29.4 0.8 copy.2040
  30.9 0.8 copy.2042
  33.1 0.8 copy.2045
  34.7 10.8 %stack.195 = bf16[27,16,2,8,128]{4,0,3,1,2:T(8,128)(2,1)S(1)} concatenate(bf16[1,16,2,8,128]{4,0,3,1,2:T(2,128)(2,1)S(1)} %copy.2026, bf16[1,16,2,8,128]{4,0,3,1,2:T(2,128)(2,1)} %copy.2027, bf16[1,16,2,8,128]{4,0,3,1,2:T(2,128)(2,1)} %copy.2028, bf16[1,16,2,8,128]{4,0,3,1,2:T(2,128)(2,1)} %copy.2029, bf16[1,16,2,8,128]{4,0,3,1,2:T(2,128)(2,1)S(1)} %copy.2030, ...), dimensions={0} | concatenate | bytes 3538944 | tf_op jit(solution)/shard_map/stack | solution.py:45
  45.5 1.9 copy.2053
  47.4 3.8 %reshape.339 = bf16[432,2048]{1,0:T(8,128)(2,1)} reshape(bf16[27,16,2,8,128]{4,3,2,1,0:T(8,128)(2,1)} %copy.2053) | data formatting | bytes 3538944 | tf_op jit(solution)/shard_map/reshape | solution.py:45
  51.2 2.6 %convolution_convert_fusion = bf16[32,2048]{1,0:T(8,128)(2,1)} fusion(bf16[32,432]{0,1:T(8,128)(2,1)S(1)} %bitcast.368, bf16[432,2048]{1,0:T(8,128)(2,1)} %reshape.339), kind=kOutput, calls=%fused_computation | convolution fusion | flops 56688640 | bytes 1928192 | tf_op jit(solution)/shard_map/dot_general | solution.py:106
  53.9 9.7 %reduce-scatter.3.cloned.1.call-done = bf16[16,2048]{1,0:T(8,128)(2,1)} async-done(((bf16[32,2048]{1,0:T(8,128)(2,1)}), bf16[16,2048]{1,0:T(8,128)(2,1)}) %reduce-scatter.3.cloned.1.call-update) | async-done | bytes 65552 | tf_op jit(solution)/shard_map/reduce_scatter | solution.py:107
  63.6 1.5 fusion.28
  65.2 1.2 copy.2054
  66.4 1.6 reduce_sum.9
  68.0 0.9 multiply_convert_fusion
  69.0 1.3 collective-permute-start.3
  70.3 4.5 %collective-permute-start.2 = (bf16[16,1,4,64]{3,2,0,1:T(4,128)(2,1)S(1)}, bf16[16,1,4,64]{3,2,0,1:T(4,128)(2,1)S(1)}, u32[]{:S(2)}, u32[]{:S(2)}) collective-permute-start(bf16[16,1,4,64]{3,2,0,1:T(4,128)(2,1)S(1)} %bitcast.399), channel_id=1, source_target_pairs={{0,2},{2,4},{4,6},{6,8},{8,10},{10,12},{12,14},{14,16},{16,18},{18... | collective-permute-start | bytes 24584 | tf_op jit(solution)/shard_map/ppermute | solution.py:16
  74.9 1.4 collective-permute-done.2
  78.7 0.8 convolution_convert_fusion.1
  79.7 11.3 %reduce-scatter.5.cloned.1.call-done = bf16[32,256]{1,0:T(8,128)(2,1)} async-done(((bf16[64,256]{1,0:T(8,128)(2,1)}), bf16[32,256]{1,0:T(8,128)(2,1)}) %reduce-scatter.5.cloned.1.call-update) | async-done | bytes 16400 | tf_op jit(solution)/shard_map/reduce_scatter | solution.py:121
  91.8 1.3 collective-permute-start.5
  93.1 4.5 %collective-permute-start.4 = (bf16[32,1,4,64]{3,0,2,1:T(8,128)(2,1)S(1)}, bf16[32,1,4,64]{3,0,2,1:T(8,128)(2,1)S(1)}, u32[]{:S(2)}, u32[]{:S(2)}) collective-permute-start(bf16[32,1,4,64]{3,0,2,1:T(8,128)(2,1)S(1)} %copy.2056), channel_id=1, source_target_pairs={{0,2},{2,4},{4,6},{6,8},{8,10},{10,12},{12,14},{14,16},{16,18},{18... | collective-permute-start | bytes 49160 | tf_op jit(solution)/shard_map/ppermute | solution.py:16
  97.7 1.6 collective-permute-done.4
  99.3 2.1 all_gather.6
  104.3 1.0 fusion.95
  106.2 0.9 fusion.53
  107.2 4.5 %collective-permute-start.6 = (bf16[16,1,8,128]{3,0,2,1:T(8,128)(2,1)S(1)}, bf16[16,1,8,128]{3,0,2,1:T(8,128)(2,1)S(1)}, u32[]{:S(2)}, u32[]{:S(2)}) collective-permute-start(bf16[16,1,8,128]{3,0,2,1:T(8,128)(2,1)S(1)} %get-tuple-element.144), channel_id=1, source_target_pairs={{0,2},{2,4},{4,6},{6,8},{8,10},{10,12},{12,14},{14,16},{16,18},{18... | collective-permute-start | bytes 98312 | tf_op jit(solution)/shard_map/ppermute | solution.py:16
  111.7 1.3 collective-permute-start.7
  113.0 2.1 convolution_bitcast_fusion
  115.2 3.5 %collective-permute-done.7 = bf16[16,1,8,128]{3,0,2,1:T(8,128)(2,1)S(1)} collective-permute-done((bf16[16,1,8,128]{3,0,2,1:T(8,128)(2,1)S(1)}, bf16[16,1,8,128]{3,0,2,1:T(8,128)(2,1)S(1)}, u32[]{:S(2)}, u32[]{:S(2)}) %collective-permute-start.7) | collective-permute-done | bytes 32800 | tf_op jit(solution)/shard_map/ppermute | solution.py:19
  118.8 2.0 all_gather.7
  122.2 1.6 reshape.344
  123.8 2.8 %dot_general.32 = bf16[4,10,130,32]{2,1,0,3:T(8,128)(2,1)S(1)} reshape(bf16[5200,32]{0,1:T(8,128)(2,1)} %bitcast.366) | data formatting | bytes 665600 | tf_op jit(solution)/shard_map/dot_general | solution.py:68
  126.7 2.5 %fusion = f32[27,16,4,10,130]{4,1,3,2,0:T(8,128)S(1)} fusion(bf16[4,10,130,32]{2,1,0,3:T(8,128)(2,1)S(1)} %dot_general.32, bf16[32,16,27]{0,1,2:T(8,128)(2,1)S(1)} %copy-done.6), kind=kOutput, calls=%fused_computation.28 | convolution fusion | flops 143769600 | bytes 9346048 | tf_op jit(solution)/shard_map/dot_general | solution.py:68
  130.1 1.7 convolution_bitcast_fusion.1
  131.8 77.8 %psum.14 = f32[32,16,27]{2,0,1:T(8,128)S(1)} all-reduce(f32[32,16,27]{2,0,1:T(8,128)S(1)} %convolution_bitcast_fusion.1), channel_id=1, replica_groups=mesh['depth'=16,'chan'=2] {'depth'}, use_global_device_ids=true, to_apply=%region_3.4 | all-reduce | flops 13824 | bytes 110592 | tf_op jit(solution)/shard_map/psum | solution.py:154
  209.6 0.9 copy.2096
  211.1 17.6 %all-reduce.6.cloned.1.call-done = f32[64,16,27]{0,2,1:T(8,128)} async-done(((f32[64,16,27]{0,2,1:T(8,128)}), f32[64,16,27]{0,2,1:T(8,128)}) %all-reduce.6.cloned.1.call-update) | async-done | bytes 110608 | tf_op jit(solution)/shard_map/psum | solution.py:135
  228.8 1.8 copy.2097
  (104 shorter events, 18.7 us)
Async XLA Ops:
  7.2 46.7 %copy-start = (bf16[64,32,27]{0,1,2:T(8,128)(2,1)S(1)}, bf16[64,32,27]{0,1,2:T(8,128)(2,1)}, u32[]{:S(2)}) copy-start(bf16[64,32,27]{0,1,2:T(8,128)(2,1)} %param.6) | copy-start | bytes 331780
  7.2 56.4 %reduce-scatter.3.cloned.1.call-start = ((), (), s32[]{:S(2)}) async-start(), calls=%async_computation.2 | async-start | bytes 196608 | tf_op jit(solution)/shard_map/reduce_scatter | solution.py:107
  8.2 7.4 %collective-permute-start = (bf16[16,1,8,128]{3,0,2,1:T(8,128)(2,1)S(1)}, bf16[16,1,8,128]{3,0,2,1:T(8,128)(2,1)S(1)}, u32[]{:S(2)}, u32[]{:S(2)}) collective-permute-start(bf16[16,1,8,128]{3,0,2,1:T(8,128)(2,1)S(1)} %get-tuple-element.146), channel_id=1, source_target_pairs={{0,2},{2,4},{4,6},{6,8},{8,10},{10,12},{12,14},{14,16},{16,18},{18... | collective-permute-start | bytes 98312 | tf_op jit(solution)/shard_map/ppermute | solution.py:16
  13.0 5.8 %collective-permute-start.1 = (bf16[16,1,8,128]{3,0,2,1:T(8,128)(2,1)S(1)}, bf16[16,1,8,128]{3,0,2,1:T(8,128)(2,1)S(1)}, u32[]{:S(2)}, u32[]{:S(2)}) collective-permute-start(bf16[16,1,8,128]{3,0,2,1:T(8,128)(2,1)S(1)} %get-tuple-element.147), channel_id=1, source_target_pairs={{2,0},{4,2},{6,4},{8,6},{10,8},{12,10},{14,12},{16,14},{18,16},{20... | collective-permute-start | bytes 98312 | tf_op jit(solution)/shard_map/ppermute | solution.py:19
  15.6 35.7 %copy-start.5 = (bf16[32,16,27]{0,1,2:T(8,128)(2,1)}, bf16[32,16,27]{0,1,2:T(8,128)(2,1)S(1)}, u32[]{:S(2)}) copy-start(bf16[32,16,27]{0,1,2:T(8,128)(2,1)S(1)} %copy.2157) | copy-start | bytes 82948
  53.9 37.1 %reduce-scatter.5.cloned.1.call-start = ((), (), s32[]{:S(2)}) async-start(), calls=%async_computation.3 | async-start | bytes 49152 | tf_op jit(solution)/shard_map/reduce_scatter | solution.py:121
  66.4 13.2 %copy-start.7 = (bf16[32,1,4,64]{3,2,1,0:T(4,128)(2,1)S(1)}, bf16[32,1,4,64]{3,2,1,0:T(4,128)(2,1)}, u32[]{:S(2)}) copy-start(bf16[32,1,4,64]{3,2,1,0:T(4,128)(2,1)} %param.7) | copy-start | bytes 49156
  69.0 5.9 %collective-permute-start.3 = (bf16[16,1,4,64]{3,2,0,1:T(4,128)(2,1)S(1)}, bf16[16,1,4,64]{3,2,0,1:T(4,128)(2,1)S(1)}, u32[]{:S(2)}, u32[]{:S(2)}) collective-permute-start(bf16[16,1,4,64]{3,2,0,1:T(4,128)(2,1)S(1)} %bitcast.398), channel_id=1, source_target_pairs={{2,0},{4,2},{6,4},{8,6},{10,8},{12,10},{14,12},{16,14},{18,16},{20... | collective-permute-start | bytes 24584 | tf_op jit(solution)/shard_map/ppermute | solution.py:19
  70.3 6.0 %collective-permute-start.2 = (bf16[16,1,4,64]{3,2,0,1:T(4,128)(2,1)S(1)}, bf16[16,1,4,64]{3,2,0,1:T(4,128)(2,1)S(1)}, u32[]{:S(2)}, u32[]{:S(2)}) collective-permute-start(bf16[16,1,4,64]{3,2,0,1:T(4,128)(2,1)S(1)} %bitcast.399), channel_id=1, source_target_pairs={{0,2},{2,4},{4,6},{6,8},{8,10},{10,12},{12,14},{14,16},{16,18},{18... | collective-permute-start | bytes 24584 | tf_op jit(solution)/shard_map/ppermute | solution.py:16
  78.3 25.5 %copy-start.1 = (bf16[27,16,1,4,64]{4,3,1,2,0:T(4,128)(2,1)}, bf16[27,16,1,4,64]{4,3,1,2,0:T(4,128)(2,1)S(1)}, u32[]{:S(2)}) copy-start(bf16[27,16,1,4,64]{4,3,1,2,0:T(4,128)(2,1)S(1)} %constant_dynamic-update-slice_fusion) | copy-start | bytes 663556
  79.5 149.2 %all-reduce.6.cloned.1.call-start = ((), (), s32[]{:S(2)}) async-start(), calls=%async_computation.4 | async-start | bytes 524288 | tf_op jit(solution)/shard_map/psum | solution.py:135
  91.8 5.9 %collective-permute-start.5 = (bf16[32,1,4,64]{3,0,2,1:T(8,128)(2,1)S(1)}, bf16[32,1,4,64]{3,0,2,1:T(8,128)(2,1)S(1)}, u32[]{:S(2)}, u32[]{:S(2)}) collective-permute-start(bf16[32,1,4,64]{3,0,2,1:T(8,128)(2,1)S(1)} %copy.2056), channel_id=1, source_target_pairs={{2,0},{4,2},{6,4},{8,6},{10,8},{12,10},{14,12},{16,14},{18,16},{20... | collective-permute-start | bytes 49160 | tf_op jit(solution)/shard_map/ppermute | solution.py:19
  93.1 6.1 %collective-permute-start.4 = (bf16[32,1,4,64]{3,0,2,1:T(8,128)(2,1)S(1)}, bf16[32,1,4,64]{3,0,2,1:T(8,128)(2,1)S(1)}, u32[]{:S(2)}, u32[]{:S(2)}) collective-permute-start(bf16[32,1,4,64]{3,0,2,1:T(8,128)(2,1)S(1)} %copy.2056), channel_id=1, source_target_pairs={{0,2},{2,4},{4,6},{6,8},{8,10},{10,12},{12,14},{14,16},{16,18},{18... | collective-permute-start | bytes 49160 | tf_op jit(solution)/shard_map/ppermute | solution.py:16
  101.4 0.7 copy-start.4
  107.2 7.9 %collective-permute-start.6 = (bf16[16,1,8,128]{3,0,2,1:T(8,128)(2,1)S(1)}, bf16[16,1,8,128]{3,0,2,1:T(8,128)(2,1)S(1)}, u32[]{:S(2)}, u32[]{:S(2)}) collective-permute-start(bf16[16,1,8,128]{3,0,2,1:T(8,128)(2,1)S(1)} %get-tuple-element.144), channel_id=1, source_target_pairs={{0,2},{2,4},{4,6},{6,8},{8,10},{10,12},{12,14},{14,16},{16,18},{18... | collective-permute-start | bytes 98312 | tf_op jit(solution)/shard_map/ppermute | solution.py:16
  111.7 7.0 %collective-permute-start.7 = (bf16[16,1,8,128]{3,0,2,1:T(8,128)(2,1)S(1)}, bf16[16,1,8,128]{3,0,2,1:T(8,128)(2,1)S(1)}, u32[]{:S(2)}, u32[]{:S(2)}) collective-permute-start(bf16[16,1,8,128]{3,0,2,1:T(8,128)(2,1)S(1)} %get-tuple-element.145), channel_id=1, source_target_pairs={{2,0},{4,2},{6,4},{8,6},{10,8},{12,10},{14,12},{16,14},{18,16},{20... | collective-permute-start | bytes 98312 | tf_op jit(solution)/shard_map/ppermute | solution.py:19
  120.8 0.7 copy-start.2
  121.6 5.1 %copy-start.6 = (bf16[32,16,27]{0,1,2:T(8,128)(2,1)S(1)}, bf16[32,16,27]{0,1,2:T(8,128)(2,1)}, u32[]{:S(2)}) copy-start(bf16[32,16,27]{0,1,2:T(8,128)(2,1)} %copy-done.5) | copy-start | bytes 82948
  129.2 1.0 copy-start.3
Sparse Core Ops, SparseCore 0:
  54.0 9.5 reduce-scatter.2
  79.6 11.2 reduce-scatter.4
  115.3 113.4 all-reduce.5
where the time goes:
time: 239 us; the launch traced here: 237 us
  blocking collectives  81.9 us (34%)
  local copies, waits for them, and re-layouts  51.5 us (22%)
  waiting for transfers between devices  48.4 us (20%)
  starting transfers between devices  23.7 us (10%)
  between operations  14.3 us (6%)
  matrix products  10.5 us (4%)
  other arithmetic  6.83 us (3%)
    psum x1, blocking collectives, shards(): grad_weight_one = lax.psum(grad_weight_one, 'depth')  77.8 us
    another operation x32, local copies, waits for them, and re-layouts, patch_rows(): return jnp.stack(windows, 0).reshape(27 * chans, planes * height * across)  28.5 us
    ppermute x4, starting transfers between devices, padded_2(): lax.ppermute(lax.slice_in_dim(block, block.shape[dim] - width, None, axis...  18.4 us
    psum x1, waiting for transfers between devices, shards(): grad_weight_two = lax.psum(grad_weight_two, 'depth')  17.6 us
    reduce_scatter x1, waiting for transfers between devices, shards(): lax.psum_scatter(partial_two.astype(jnp.bfloat16), 'chan', scatter_dimens...  11.3 us
    reduce_scatter x1, waiting for transfers between devices, shards(): lax.psum_scatter(partial_one.astype(jnp.bfloat16), 'chan', scatter_dimens...  9.68 us
    unnamed x51, local copies, waits for them, and re-layouts  8.2 us
    ppermute x4, waiting for transfers between devices, padded_2(): lax.ppermute(lax.slice_in_dim(block, 0, width, axis=dim), axis, backward)  6.79 us
  transfers between devices with their start and end apart: 11, of which 7 were waited for; matrix products, arithmetic and copies ran while one was open for 6% of the time, Pallas kernels for 0%

commit v1 on v0

v1 whole, which is shorter than its diff:
```python
import functools

import jax
import jax.numpy as jnp
from jax import lax
from jax.experimental import pallas as pl
from jax.experimental.pallas import tpu as pltpu
from jax.sharding import PartitionSpec as P

MESH = pl.DeviceIdType.MESH
BF16 = jnp.bfloat16
F32 = jnp.float32


def dot(left, right):
    return jnp.dot(left, right, preferred_element_type=F32)


def dot_nt(left, right):
    return lax.dot_general(left, right, (((1,), (1,)), ((), ())), preferred_element_type=F32)


def slope(pre):
    sig = jax.nn.sigmoid(pre)
    return sig * (1.0 + pre * (1.0 - sig))


def plane_taps(field, across):
    chans, cells = field.shape
    wide = field.astype(F32)
    cell = lax.broadcasted_iota(jnp.int32, (chans, cells), 1)
    column = lax.rem(cell, across)
    moved = [
        jnp.where(column == 0, 0.0, pltpu.roll(wide, 1, 1)),
        wide,
        jnp.where(column == across - 1, 0.0, pltpu.roll(wide, cells - 1, 1)),
    ]
    if across % 128 == 0:
        moved = [m.astype(BF16) for m in moved]
        edge = jnp.zeros((chans, across), BF16)
        above = [jnp.concatenate([edge, m[:, :-across]], axis=1) for m in moved]
        below = [jnp.concatenate([m[:, across:], edge], axis=1) for m in moved]
        return above + moved + below
    above = [jnp.where(cell < across, 0.0, pltpu.roll(m, across, 1)) for m in moved]
    below = [
        jnp.where(cell >= cells - across, 0.0, pltpu.roll(m, cells - across, 1)) for m in moved
    ]
    return [m.astype(BF16) for m in above + moved + below]


def kernel(
    n, owners, across,
    feats, cot, w1f, w1b, w2f, w2b,
    out_feats, out_one, out_two,
    halo, cots, pools, x1, x2, xg1, xg2, slopes, shrink, spread,
    part1, land1, full1, part2, land2, full2,
    send_f, recv_f, send_c, recv_c, send_p, recv_p,
    send_r1, recv_r1, send_a1, recv_a1, send_r2, recv_r2, send_a2, recv_a2,
):
    place = lax.axis_index("depth")
    core = lax.axis_index("chan")
    other = 1 - core
    half = feats.shape[1]
    cells = feats.shape[2]
    small = cot.shape[1]
    rows1 = 9 * half
    stride = n // owners

    def at(step):
        return lax.rem(place + step + n, n)

    barrier = pltpu.get_barrier_semaphore()

    def greet(device):
        pl.semaphore_signal(barrier, inc=1, device_id=device, device_id_type=MESH)

    greet((place, other))
    for step in (1, -1, 2, -2):
        greet((at(step), other))

    def greet_row(step, carry):
        greet((at(step), core))
        return carry

    lax.fori_loop(1, n, greet_row, 0)

    def valid(step):
        return jnp.logical_and(place + step >= 0, place + step < n)

    def put_x1(plane, side, field):
        for tap, block in enumerate(plane_taps(field, across)):
            x1[side, pl.ds(plane * rows1 + tap * half, half), :] = block

    big_row = lax.broadcasted_iota(jnp.int32, (cells, small), 0)
    small_col = lax.broadcasted_iota(jnp.int32, (cells, small), 1)
    target = (big_row // (2 * across)) * (across // 2) + lax.rem(big_row, across) // 2
    shrink[...] = jnp.where(target == small_col, 0.125, 0.0).astype(BF16)
    big_col = lax.broadcasted_iota(jnp.int32, (small, cells), 1)
    small_row = lax.broadcasted_iota(jnp.int32, (small, cells), 0)
    target = (big_col // (2 * across)) * (across // 2) + lax.rem(big_col, across) // 2
    spread[...] = jnp.where(target == small_row, 0.125, 0.0).astype(BF16)

    for plane in range(2):
        put_x1(2 + plane, core, feats[plane])
    cots[2, core] = cot[...]

    pl.semaphore_wait(barrier, n + 4)

    def copy(src, dst, send, recv, device):
        return pltpu.make_async_remote_copy(
            src_ref=src, dst_ref=dst, send_sem=send, recv_sem=recv,
            device_id=device, device_id_type=MESH,
        )

    near, far = [], []
    mate = copy(feats, halo.at[pl.ds(2, 2), core], send_f.at[0], recv_f.at[0], (place, other))
    mate.start()
    index = 1
    for planes in ((1, 0), (0, 1)):
        for step, plane in zip((1, -1), planes):
            for who in (core, other):
                to = plane if step == 1 else 4 + plane
                one = copy(
                    feats.at[plane], halo.at[to, core], send_f.at[index], recv_f.at[index],
                    (at(step), who),
                )
                one.start()
                (near if index < 5 else far).append(one)
                index += 1
    cot_copies = []
    index = 0
    targets = [(0, other)] + [(s, w) for s in (1, -1, 2, -2) for w in (core, other)]
    for step, who in targets:
        one = copy(
            cot, cots.at[2 - step, core], send_c.at[index], recv_c.at[index], (at(step), who)
        )
        one.start()
        cot_copies.append(one)
        index += 1

    def take_halo(plane, side, keep):
        field = halo[plane, side]
        if keep is not None:
            field = jnp.where(keep, field.astype(F32), 0.0)
        put_x1(plane, side, field)

    def conv_one(plane):
        total = dot(w1f[0], x1[0, (plane - 1) * rows1 : (plane + 2) * rows1, :])
        return total + dot(w1f[1], x1[1, (plane - 1) * rows1 : (plane + 2) * rows1, :])

    mate.wait_recv()
    for plane in (2, 3):
        take_halo(plane, other, None)
    for one in near:
        one.wait_recv()
    for plane, step in ((1, -1), (4, 1)):
        for side in range(2):
            take_halo(plane, side, valid(step))

    pooled = None
    for plane in (2, 3):
        pre = conv_one(plane)
        sig = jax.nn.sigmoid(pre)
        slopes[plane - 1] = sig * (1.0 + pre * (1.0 - sig))
        term = dot((pre * sig).astype(BF16), shrink[...])
        pooled = term if pooled is None else pooled + term
    pools[3] = pooled.astype(BF16)
    pool_copies = []
    for index, step in enumerate((1, -1, 2, -2, 3, -3)):
        one = copy(
            pools.at[3], pools.at[3 - step], send_p.at[index], recv_p.at[index], (at(step), core)
        )
        one.start()
        pool_copies.append(one)

    for one in far:
        one.wait_recv()
    for plane, step in ((0, -1), (5, 1)):
        for side in range(2):
            take_halo(plane, side, valid(step))
    for plane in (1, 4):
        slopes[plane - 1] = slope(conv_one(plane))

    def put_x2(plane, keep):
        field = pools[plane].astype(F32)
        if keep is not None:
            field = jnp.where(keep, field, 0.0)
        for tap, block in enumerate(plane_taps(field, across // 2)):
            for side in range(2):
                x2[side, pl.ds(plane * rows1 + tap * half, half), :] = block[
                    side * half : (side + 1) * half
                ]

    put_x2(3, None)
    for one in cot_copies:
        one.wait_recv()
    for one in pool_copies:
        one.wait_recv()
    for plane in (2, 4, 1, 5, 0, 6):
        put_x2(plane, valid(plane - 3))

    outs = 2 * cot.shape[0]
    rows2 = 9 * outs
    own_grad = None
    for plane in range(5):
        pre = dot(w2f[0], x2[0, plane * rows1 : (plane + 3) * rows1, :])
        pre = pre + dot(w2f[1], x2[1, plane * rows1 : (plane + 3) * rows1, :])
        grad = cots[plane].reshape(outs, small).astype(F32) * slope(pre)
        if plane != 2:
            grad = jnp.where(valid(plane - 2), grad, 0.0)
        else:
            own_grad = grad.astype(BF16)
        grad = grad.astype(BF16)
        for tap, block in enumerate(plane_taps(grad, across // 2)):
            xg2[pl.ds(plane * rows2 + tap * outs, outs), :] = block

    lanes = 512
    mine = place // stride
    is_owner = lax.rem(place, stride) == 0

    def when_owner(body):
        if stride == 1:
            body()
        else:
            pl.when(is_owner)(body)

    def chunk_out(total, part):
        rows = part.shape[1]
        for chunk in range(owners):
            r, l = chunk // 4, chunk % 4
            part[chunk] = total[r * rows : (r + 1) * rows, l * 128 : (l + 1) * 128].astype(BF16)

    def scatter_copy(part, land, send, recv, chunk, source, device):
        return copy(part.at[chunk], land.at[source], send.at[chunk], recv.at[source], device)

    def scatter(part, land, send, recv):
        def go(step, carry):
            chunk = lax.rem(mine + step, owners)

            @pl.when(chunk * stride != place)
            def _():
                scatter_copy(part, land, send, recv, chunk, place, (chunk * stride, core)).start()

            return carry

        lax.fori_loop(0, owners, go, 0)

        @when_owner
        def _():
            land[place] = part[mine]

    def gather(part, land, full, recv_r, send, recv):
        @when_owner
        def _():
            def arrived(step, carry):
                source = at(step)
                scatter_copy(part, land, send, recv_r, 0, source, (place, other)).wait_recv()
                return carry

            lax.fori_loop(1, n, arrived, 0)
            full[mine] = jnp.sum(land[...].astype(F32), axis=0).astype(BF16)

            def go(step, carry):
                copy(
                    full.at[mine], full.at[mine], send.at[at(step)], recv.at[mine], (at(step), core)
                ).start()
                return carry

            lax.fori_loop(1, n, go, 0)

    def finish(part, land, full, send_r, send, recv, out):
        def came(chunk, carry):
            @pl.when(chunk * stride != place)
            def _():
                copy(
                    full.at[chunk], full.at[chunk], send.at[0], recv.at[chunk], (place, other)
                ).wait_recv()
                scatter_copy(part, land, send_r, recv, chunk, 0, (place, other)).wait_send()

            return carry

        lax.fori_loop(0, owners, came, 0)

        @when_owner
        def _():
            def sent(step, carry):
                copy(
                    full.at[mine], full.at[mine], send.at[at(step)], recv.at[0], (place, other)
                ).wait_send()
                return carry

            lax.fori_loop(1, n, sent, 0)

        rows = part.shape[1]
        for chunk in range(owners):
            r, l = chunk // 4, chunk % 4
            out[r * rows : (r + 1) * rows, l * 128 : (l + 1) * 128] = full[chunk].astype(F32)

    total2 = dot_nt(own_grad, x2[core, 2 * rows1 : 2 * rows1 + lanes, :])
    chunk_out(total2, part2)
    scatter(part2, land2, send_r2, recv_r2)

    grads = []
    for plane in range(3):
        back = dot(w2b[...], xg2[plane * rows2 : (plane + 3) * rows2, :]).astype(BF16)
        wide = dot(back, spread[...])
        for where in ((0,), (1, 2), (3,))[plane]:
            grad = wide * slopes[where]
            if plane != 1:
                grad = jnp.where(valid(plane - 1), grad, 0.0)
            grads.append(grad.astype(BF16))

    total1 = dot_nt(grads[1], x1[core, rows1 : rows1 + lanes, :])
    total1 = total1 + dot_nt(grads[2], x1[core, 2 * rows1 : 2 * rows1 + lanes, :])
    chunk_out(total1, part1)
    scatter(part1, land1, send_r1, recv_r1)
    gather(part2, land2, full2, recv_r2, send_a2, recv_a2)

    mids = 2 * half
    rows_g = 9 * mids
    for plane in range(4):
        for tap, block in enumerate(plane_taps(grads[plane], across)):
            xg1[pl.ds(plane * rows_g + tap * mids, mids), :] = block
    for plane in range(2):
        out_feats[plane] = dot(w1b[core], xg1[plane * rows_g : (plane + 3) * rows_g, :]).astype(BF16)

    gather(part1, land1, full1, recv_r1, send_a1, recv_a1)
    for one in [mate] + near + far + cot_copies + pool_copies:
        one.wait_send()
    finish(part2, land2, full2, send_r2, send_a2, recv_a2, out_two)
    finish(part1, land1, full1, send_r1, send_a1, recv_a1, out_one)


def shards(feats, weight_one, weight_two, cotangent):
    n = lax.axis_size("depth")
    owners = 16
    half, planes, height, across = feats.shape
    cells = height * across
    mids = weight_one.shape[0]
    outs = weight_two.shape[0]
    small = cells // 4
    x = jnp.transpose(feats.reshape(half, planes, cells), (1, 0, 2))
    cot = cotangent.reshape(outs // 2, small)

    def forward(weight):
        o = weight.shape[0]
        return jnp.transpose(weight.reshape(o, 2, half, 27), (1, 0, 3, 2)).reshape(2, o, 27 * half)

    def backward(weight):
        return jnp.transpose(weight[:, :, ::-1], (1, 2, 0)).reshape(weight.shape[1], -1)

    w1f, w2f = forward(weight_one), forward(weight_two)
    w1b = backward(weight_one).reshape(2, half, 27 * mids)
    w2b = backward(weight_two)
    vmem = pl.BlockSpec(memory_space=pltpu.VMEM)
    dma = pltpu.SemaphoreType.DMA
    out_feats, out_one, out_two = pl.pallas_call(
        functools.partial(kernel, n, owners, across),
        out_shape=(
            jax.ShapeDtypeStruct((planes, half, cells), BF16),
            jax.ShapeDtypeStruct((mids, 512), F32),
            jax.ShapeDtypeStruct((outs, 512), F32),
        ),
        in_specs=[vmem] * 6,
        out_specs=(vmem,) * 3,
        scratch_shapes=[
            pltpu.VMEM((6, 2, half, cells), BF16),
            pltpu.VMEM((5, 2, outs // 2, small), BF16),
            pltpu.VMEM((7, mids, small), BF16),
            pltpu.VMEM((2, 6 * 9 * half, cells), BF16),
            pltpu.VMEM((2, 7 * 9 * half, small), BF16),
            pltpu.VMEM((4 * 9 * mids, cells), BF16),
            pltpu.VMEM((5 * 9 * outs, small), BF16),
            pltpu.VMEM((4, mids, cells), F32),
            pltpu.VMEM((cells, small), BF16),
            pltpu.VMEM((small, cells), BF16),
            pltpu.VMEM((owners, mids // 4, 128), BF16),
            pltpu.VMEM((n, mids // 4, 128), BF16),
            pltpu.VMEM((owners, mids // 4, 128), BF16),
            pltpu.VMEM((owners, outs // 4, 128), BF16),
            pltpu.VMEM((n, outs // 4, 128), BF16),
            pltpu.VMEM((owners, outs // 4, 128), BF16),
            dma((9,)), dma((9,)), dma((9,)), dma((9,)), dma((6,)), dma((6,)),
            dma((owners,)), dma((n,)), dma((n,)), dma((owners,)),
            dma((owners,)), dma((n,)), dma((n,)), dma((owners,)),
        ],
        compiler_params=pltpu.CompilerParams(
            collective_id=0, has_side_effects=True, vmem_limit_bytes=60 * 1024 * 1024
        ),
    )(x, cot, w1f, w1b, w2f, w2b)

    def layout(total):
        rows = total.shape[0]
        return jnp.transpose(total[:, : 27 * half].reshape(rows, 27, half), (0, 2, 1))

    grad_feats = jnp.transpose(out_feats, (1, 0, 2)).reshape(half, planes, height, across)
    return grad_feats, layout(out_one), layout(out_two)


def solution(mesh):
    return jax.shard_map(
        shards,
        mesh=mesh,
        in_specs=(P("chan", "depth", None, None), P(), P(), P("chan", "depth", None, None)),
        out_specs=(P("chan", "depth", None, None), P(None, "chan", None), P(None, "chan", None)),
        check_vma=False,
    )
```

time: 239 us -> 45 us (0.19)
  blocking collectives: 81.9 us -> 0 us
  waiting for transfers between devices: 48.4 us -> 0 us
  local copies, waits for them, and re-layouts: 51.5 us -> 9.9 us
  Pallas kernels: 0 us -> 34 us
  starting transfers between devices: 23.7 us -> 0 us
  between operations: 14.3 us -> 0.72 us
  matrix products: 10.5 us -> 0 us
  other arithmetic: 6.83 us -> 0 us
    psum x1 -> x0, blocking collectives: 77.8 us -> none  [shards(): grad_weight_one = lax.psum(grad_weight_one, 'depth')]
    pallas_call x0 -> x1, Pallas kernels: none -> 34 us  [shards(): pl.pallas_call(functools.partial(kernel, n, owners, across), out_shape=(j...]
    another operation x32 -> x1, local copies, waits for them, and re-layouts: 28.5 us -> 0.86 us  [shards(): w1b = backward(weight_one).reshape(2, half, 27 * mids)]
    ppermute x8 -> x0, starting transfers between devices: 23.6 us -> none  [the longest x4 18.4 us: padded_2(): lax.ppermute(lax.slice_in_dim(block, block.shape[dim] - width, None, axis...]
    reduce_scatter x2 -> x0, waiting for transfers between devices: 21 us -> none  [the longest x1 11.3 us: shards(): lax.psum_scatter(partial_two.astype(jnp.bfloat16), 'chan', scatter_dimens...]
    psum x1 -> x0, waiting for transfers between devices: 17.6 us -> none  [shards(): grad_weight_two = lax.psum(grad_weight_two, 'depth')]
    dot_general x6 -> x0, matrix products: 10.5 us -> none  [the longest x2 3.84 us: grad_fold(): lax.dot_general(inner, patches, (((1,), (1,)), ((), ())), preferred_eleme...]
    ppermute x8 -> x0, waiting for transfers between devices: 9.76 us -> none  [the longest x4 6.79 us: padded_2(): lax.ppermute(lax.slice_in_dim(block, 0, width, axis=dim), axis, backward)]
  transfers between devices with their start and end apart: 11 -> 0, of which waited for: 7 -> 0; matrix products, arithmetic and copies ran while one was open for 6% -> 0% of each run, Pallas kernels for 0% -> 0%
where the time goes in v1:
time: 45 us; the launch traced here: 44.6 us
  Pallas kernels  34 us (76%)
  local copies, waits for them, and re-layouts  9.9 us (22%)
  between operations  0.72 us (2%)
    pallas_call x1, Pallas kernels, shards(): pl.pallas_call(functools.partial(kernel, n, owners, across), out_shape=(j...  34 us
    slice x2, local copies, waits for them, and re-layouts, layout(): total[:, :27 * half].reshape(rows, 27, half)  2.51 us
    reshape x2, local copies, waits for them, and re-layouts, forward(): jnp.transpose(weight.reshape(o, 2, half, 27), (1, 0, 3, 2))  1.53 us
    transpose x4, local copies, waits for them, and re-layouts, backward(): jnp.transpose(weight[:, :, ::-1], (1, 2, 0)).reshape(weight.shape[1], -1)  1.5 us
    unnamed x15, local copies, waits for them, and re-layouts  1.21 us

profile of v1, /device:TPU:0, one launch (start us, length us, event | category | flops | bytes accessed | tf_op | source)
XLA Modules:
  0.0 44.6 jit_solution(17821351445556571810)
XLA Ops:
  0.6 1.0 %reverse_bitcast_fusion = bf16[32,27,64]{2,0,1:T(8,128)(2,1)S(1)} fusion(bf16[64,32,27]{0,1,2:T(8,128)(2,1)} %param.6), kind=kLoop, calls=%fused_computation | loop fusion | bytes 221184 | tf_op jit(solution)/shard_map/transpose | solution.py:350
  1.6 0.1 copy.20
  1.7 0.0 copy-start
  1.7 0.9 %reshape.42.w2b = bf16[32,1728]{1,0:T(8,128)(2,1)} reshape(bf16[32,27,64]{2,1,0:T(8,128)(2,1)S(1)} %copy.20) | data formatting | bytes 221184 | tf_op jit(solution)/shard_map/reshape | solution.py:350
  2.6 0.0 copy-done
  2.6 0.4 copy.18
  3.1 0.9 %reshape_reshape.3.w1b = bf16[2,16,864]{2,1,0:T(8,128)(2,1)} reshape(bf16[32,27,32]{2,1,0:T(8,128)(2,1)S(1)} %copy.18) | data formatting | bytes 110592 | tf_op jit(solution)/shard_map/reshape;reshape | solution.py:353
  3.9 0.2 copy.16
  4.1 0.0 copy-start.1
  4.1 0.7 %copy.21.w1f = bf16[2,32,432]{2,1,0:T(8,128)(2,1)} copy(bf16[2,32,432]{1,2,0:T(8,128)(2,1)S(1)} %bitcast.33) | data formatting | bytes 110592 | tf_op jit(solution)/shard_map/reshape | solution.py:347
  4.9 0.2 copy-done.1
  5.1 0.0 copy-start.3
  5.1 0.8 %copy.22.w2f = bf16[2,64,432]{2,1,0:T(8,128)(2,1)} copy(bf16[2,64,432]{1,2,0:T(8,128)(2,1)S(1)} %bitcast.35) | data formatting | bytes 221184 | tf_op jit(solution)/shard_map/reshape | solution.py:347
  5.9 0.0 copy-done.3
  6.0 0.0 copy-start.5
  6.0 0.6 %copy.29 = bf16[16,2,1024]{2,0,1:T(8,128)(2,1)} copy(bf16[16,2,1024]{2,1,0:T(2,128)(2,1)S(1)} %reshape.46) | data formatting | bytes 131072 | tf_op jit(solution)/shard_map/reshape | solution.py:342
  6.6 0.1 copy-done.5
  6.7 0.7 %reshape.37.cot = bf16[32,256]{1,0:T(8,128)(2,1)} reshape(bf16[32,1,4,64]{3,2,1,0:T(4,128)(2,1)S(1)} %copy-done.5) | data formatting | bytes 32768 | tf_op jit(solution)/shard_map/reshape | solution.py:343
  7.4 34.0 %shard_map.67 = (bf16[2,16,1024]{2,1,0:T(8,128)(2,1)}, f32[32,512]{1,0:T(8,128)}, f32[64,512]{1,0:T(8,128)}) custom-call(bf16[2,16,1024]{2,1,0:T(8,128)(2,1)} %bitcast.36, bf16[32,256]{1,0:T(8,128)(2,1)} %reshape.37.cot, bf16[2,32,432]{2,1,0:T(8,128)(2,1)} %copy.21.w1f, bf16[2,16,864]{2,1,0:T(8,128)(2,1)} %reshape_reshape.3.w1b, ...), custom_call_target="tpu_custom_call" | custom-call | tf_op jit(solution)/shard_map/pallas_call | solution.py:357
  41.4 0.0 copy-start.2
  41.4 1.7 %copy.23 = f32[32,432]{0,1:T(8,128)} copy(f32[32,432]{1,0:T(8,128)} %bitcast.42) | data formatting | bytes 110592 | tf_op jit(solution)/shard_map/slice | solution.py:394
  43.1 0.0 copy-done.2
  43.1 0.0 copy-start.4
  43.1 0.8 %copy.24 = f32[64,432]{0,1:T(8,128)} copy(f32[64,432]{1,0:T(8,128)S(1)} %bitcast.40) | data formatting | bytes 221184 | tf_op jit(solution)/shard_map/slice | solution.py:394
  43.9 0.0 copy-done.4
  43.9 0.6 %copy.25 = bf16[16,2,8,128]{3,2,1,0:T(8,128)(2,1)} copy(bf16[16,2,8,128]{3,2,0,1:T(8,128)(2,1)S(1)} %bitcast.37) | data formatting | bytes 131072
  (5 shorter events, 0.1 us)
Async XLA Ops:
  1.7 0.9 %copy-start = (bf16[32,32,27]{1,0,2:T(8,128)(2,1)S(1)}, bf16[32,32,27]{1,0,2:T(8,128)(2,1)}, u32[]{:S(2)}) copy-start(bf16[32,32,27]{1,0,2:T(8,128)(2,1)} %param.5) | copy-start | bytes 165892
  4.1 0.9 %copy-start.1 = (bf16[64,32,27]{0,1,2:T(8,128)(2,1)S(1)}, bf16[64,32,27]{0,1,2:T(8,128)(2,1)}, u32[]{:S(2)}) copy-start(bf16[64,32,27]{0,1,2:T(8,128)(2,1)} %param.6) | copy-start | bytes 331780
  5.1 0.8 %copy-start.3 = (bf16[16,2,8,128]{3,2,1,0:T(8,128)(2,1)S(1)}, bf16[16,2,8,128]{3,2,1,0:T(8,128)(2,1)}, u32[]{:S(2)}) copy-start(bf16[16,2,8,128]{3,2,1,0:T(8,128)(2,1)} %param.4) | copy-start | bytes 196612
  6.0 0.8 %copy-start.5 = (bf16[32,1,4,64]{3,2,1,0:T(4,128)(2,1)S(1)}, bf16[32,1,4,64]{3,2,1,0:T(4,128)(2,1)}, u32[]{:S(2)}) copy-start(bf16[32,1,4,64]{3,2,1,0:T(4,128)(2,1)} %param.7) | copy-start | bytes 49156
  41.4 1.7 %copy-start.2 = (f32[64,512]{1,0:T(8,128)S(1)}, f32[64,512]{1,0:T(8,128)}, u32[]{:S(2)}) copy-start(f32[64,512]{1,0:T(8,128)} %get-tuple-element.8) | copy-start | bytes 393220
  43.1 0.8 %copy-start.4 = (bf16[2,16,1024]{2,1,0:T(8,128)(2,1)S(1)}, bf16[2,16,1024]{2,1,0:T(8,128)(2,1)}, u32[]{:S(2)}) copy-start(bf16[2,16,1024]{2,1,0:T(8,128)(2,1)} %get-tuple-element.6) | copy-start | bytes 196612

commit v2 on v1

--- a/solution.py
+++ b/solution.py
@@ -50,9 +50,9 @@
 
 def kernel(
     n, owners, across,
-    feats, cot, w1f, w1b, w2f, w2b,
+    feats_in, cot_in, w1, w2,
     out_feats, out_one, out_two,
-    halo, cots, pools, x1, x2, xg1, xg2, slopes, shrink, spread,
+    feats, rel, cot, crel, w1f, w1b, w2f, w2b, halo, cots, pools, x1, x2, xg1, xg2, slopes, shrink, spread,
     part1, land1, full1, part2, land2, full2,
     send_f, recv_f, send_c, recv_c, send_p, recv_p,
     send_r1, recv_r1, send_a1, recv_a1, send_r2, recv_r2, send_a2, recv_a2,
@@ -100,9 +100,31 @@
     target = (big_col // (2 * across)) * (across // 2) + lax.rem(big_col, across) // 2
     spread[...] = jnp.where(target == small_row, 0.125, 0.0).astype(BF16)
 
+    rows = cells // across
     for plane in range(2):
+        rel[plane] = feats_in[:, plane].astype(F32).reshape(half * rows, across)
+        for row in range(rows):
+            feats[plane, :, row * across : (row + 1) * across] = rel[
+                plane, pl.ds(row, half, stride=rows), :
+            ].astype(BF16)
         put_x1(2 + plane, core, feats[plane])
+    short = small // (across // 2)
+    for chan in range(cot.shape[0]):
+        crel[chan * 8 : chan * 8 + short, :] = cot_in[chan, 0].astype(F32)
+    lines = [crel[pl.ds(row, cot.shape[0], stride=8), :] for row in range(short)]
+    cot[...] = jnp.concatenate(lines, axis=1).astype(BF16)
     cots[2, core] = cot[...]
+
+    taps, mids, _ = w1.shape
+    outs = w2.shape[2]
+    for side in range(2):
+        lo, hi = side * half, (side + 1) * half
+        for tap in range(taps):
+            w1f[side, :, tap * half : (tap + 1) * half] = w1[tap][:, lo:hi]
+        w2f[side] = w2[:, lo:hi, :].reshape(taps * half, outs).T
+    w1b[...] = w1[...].reshape(taps * mids, mids).T.reshape(2, half, taps * mids)
+    for tap in range(taps):
+        w2b[:, tap * outs : (tap + 1) * outs] = w2[tap]
 
     pl.semaphore_wait(barrier, n + 4)
 
@@ -111,6 +133,17 @@
             src_ref=src, dst_ref=dst, send_sem=send, recv_sem=recv,
             device_id=device, device_id_type=MESH,
         )
+
+    def launch(one, step):
+        pl.when(valid(step))(lambda: one.start())
+
+    def arrive(pairs):
+        for one, step in pairs:
+            pl.when(valid(-step))(lambda one=one: one.wait_recv())
+
+    def leave(pairs):
+        for one, step in pairs:
+            pl.when(valid(step))(lambda one=one: one.wait_send())
 
     near, far = [], []
     mate = copy(feats, halo.at[pl.ds(2, 2), core], send_f.at[0], recv_f.at[0], (place, other))
@@ -124,8 +157,8 @@
                     feats.at[plane], halo.at[to, core], send_f.at[index], recv_f.at[index],
                     (at(step), who),
                 )
-                one.start()
-                (near if index < 5 else far).append(one)
+                launch(one, step)
+                (near if index < 5 else far).append((one, step))
                 index += 1
     cot_copies = []
     index = 0
@@ -134,8 +167,8 @@
         one = copy(
             cot, cots.at[2 - step, core], send_c.at[index], recv_c.at[index], (at(step), who)
         )
-        one.start()
-        cot_copies.append(one)
+        launch(one, step)
+        cot_copies.append((one, step))
         index += 1
 
     def take_halo(plane, side, keep):
@@ -151,8 +184,7 @@
     mate.wait_recv()
     for plane in (2, 3):
         take_halo(plane, other, None)
-    for one in near:
-        one.wait_recv()
+    arrive(near)
     for plane, step in ((1, -1), (4, 1)):
         for side in range(2):
             take_halo(plane, side, valid(step))
@@ -170,11 +202,10 @@
         one = copy(
             pools.at[3], pools.at[3 - step], send_p.at[index], recv_p.at[index], (at(step), core)
         )
-        one.start()
-        pool_copies.append(one)
-
-    for one in far:
-        one.wait_recv()
+        launch(one, step)
+        pool_copies.append((one, step))
+
+    arrive(far)
     for plane, step in ((0, -1), (5, 1)):
         for side in range(2):
             take_halo(plane, side, valid(step))
@@ -192,14 +223,11 @@
                 ]
 
     put_x2(3, None)
-    for one in cot_copies:
-        one.wait_recv()
-    for one in pool_copies:
-        one.wait_recv()
+    arrive(cot_copies)
+    arrive(pool_copies)
     for plane in (2, 4, 1, 5, 0, 6):
         put_x2(plane, valid(plane - 3))
 
-    outs = 2 * cot.shape[0]
     rows2 = 9 * outs
     own_grad = None
     for plane in range(5):
@@ -212,7 +240,7 @@
             own_grad = grad.astype(BF16)
         grad = grad.astype(BF16)
         for tap, block in enumerate(plane_taps(grad, across // 2)):
-            xg2[pl.ds(plane * rows2 + tap * outs, outs), :] = block
+            xg2[pl.ds((4 - plane) * rows2 + (8 - tap) * outs, outs), :] = block
 
     lanes = 512
     mine = place // stride
@@ -291,10 +319,11 @@
 
             lax.fori_loop(1, n, sent, 0)
 
-        rows = part.shape[1]
-        for chunk in range(owners):
-            r, l = chunk // 4, chunk % 4
-            out[r * rows : (r + 1) * rows, l * 128 : (l + 1) * 128] = full[chunk].astype(F32)
+        bands = [
+            jnp.concatenate([full[4 * r + l].astype(F32) for l in range(4)], axis=1)
+            for r in range(owners // 4)
+        ]
+        out[...] = jnp.concatenate(bands, axis=0).T[: out.shape[0]]
 
     total2 = dot_nt(own_grad, x2[core, 2 * rows1 : 2 * rows1 + lanes, :])
     chunk_out(total2, part2)
@@ -302,7 +331,7 @@
 
     grads = []
     for plane in range(3):
-        back = dot(w2b[...], xg2[plane * rows2 : (plane + 3) * rows2, :]).astype(BF16)
+        back = dot(w2b[...], xg2[(2 - plane) * rows2 : (5 - plane) * rows2, :]).astype(BF16)
         wide = dot(back, spread[...])
         for where in ((0,), (1, 2), (3,))[plane]:
             grad = wide * slopes[where]
@@ -316,17 +345,21 @@
     scatter(part1, land1, send_r1, recv_r1)
     gather(part2, land2, full2, recv_r2, send_a2, recv_a2)
 
-    mids = 2 * half
     rows_g = 9 * mids
     for plane in range(4):
         for tap, block in enumerate(plane_taps(grads[plane], across)):
-            xg1[pl.ds(plane * rows_g + tap * mids, mids), :] = block
+            xg1[pl.ds((3 - plane) * rows_g + (8 - tap) * mids, mids), :] = block
     for plane in range(2):
-        out_feats[plane] = dot(w1b[core], xg1[plane * rows_g : (plane + 3) * rows_g, :]).astype(BF16)
+        field = dot(w1b[core], xg1[(1 - plane) * rows_g : (4 - plane) * rows_g, :])
+        for row in range(rows):
+            rel[plane, pl.ds(row, half, stride=rows), :] = field[
+                :, row * across : (row + 1) * across
+            ]
+        out_feats[:, plane] = rel[plane].reshape(half, rows, across).astype(BF16)
 
     gather(part1, land1, full1, recv_r1, send_a1, recv_a1)
-    for one in [mate] + near + far + cot_copies + pool_copies:
-        one.wait_send()
+    mate.wait_send()
+    leave(near + far + cot_copies + pool_copies)
     finish(part2, land2, full2, send_r2, send_a2, recv_a2, out_two)
     finish(part1, land1, full1, send_r1, send_a1, recv_a1, out_one)
 
@@ -339,31 +372,29 @@
     mids = weight_one.shape[0]
     outs = weight_two.shape[0]
     small = cells // 4
-    x = jnp.transpose(feats.reshape(half, planes, cells), (1, 0, 2))
-    cot = cotangent.reshape(outs // 2, small)
-
-    def forward(weight):
-        o = weight.shape[0]
-        return jnp.transpose(weight.reshape(o, 2, half, 27), (1, 0, 3, 2)).reshape(2, o, 27 * half)
-
-    def backward(weight):
-        return jnp.transpose(weight[:, :, ::-1], (1, 2, 0)).reshape(weight.shape[1], -1)
-
-    w1f, w2f = forward(weight_one), forward(weight_two)
-    w1b = backward(weight_one).reshape(2, half, 27 * mids)
-    w2b = backward(weight_two)
+    taps = weight_one.shape[2]
+    w1 = jnp.transpose(weight_one, (2, 0, 1))
+    w2 = jnp.transpose(weight_two, (2, 1, 0))
     vmem = pl.BlockSpec(memory_space=pltpu.VMEM)
     dma = pltpu.SemaphoreType.DMA
     out_feats, out_one, out_two = pl.pallas_call(
         functools.partial(kernel, n, owners, across),
         out_shape=(
-            jax.ShapeDtypeStruct((planes, half, cells), BF16),
-            jax.ShapeDtypeStruct((mids, 512), F32),
-            jax.ShapeDtypeStruct((outs, 512), F32),
+            jax.ShapeDtypeStruct(feats.shape, BF16),
+            jax.ShapeDtypeStruct((taps * half, mids), F32),
+            jax.ShapeDtypeStruct((taps * half, outs), F32),
         ),
-        in_specs=[vmem] * 6,
+        in_specs=[vmem] * 4,
         out_specs=(vmem,) * 3,
         scratch_shapes=[
+            pltpu.VMEM((planes, half, cells), BF16),
+            pltpu.VMEM((planes, half * height, across), F32),
+            pltpu.VMEM((outs // 2, small), BF16),
+            pltpu.VMEM((outs // 2 * 8, across // 2), F32),
+            pltpu.VMEM((2, mids, taps * half), BF16),
+            pltpu.VMEM((2, half, taps * mids), BF16),
+            pltpu.VMEM((2, outs, taps * half), BF16),
+            pltpu.VMEM((mids, taps * outs), BF16),
             pltpu.VMEM((6, 2, half, cells), BF16),
             pltpu.VMEM((5, 2, outs // 2, small), BF16),
             pltpu.VMEM((7, mids, small), BF16),
@@ -387,14 +418,12 @@
         compiler_params=pltpu.CompilerParams(
             collective_id=0, has_side_effects=True, vmem_limit_bytes=60 * 1024 * 1024
         ),
-    )(x, cot, w1f, w1b, w2f, w2b)
+    )(feats, cotangent, w1, w2)
 
     def layout(total):
-        rows = total.shape[0]
-        return jnp.transpose(total[:, : 27 * half].reshape(rows, 27, half), (0, 2, 1))
-
-    grad_feats = jnp.transpose(out_feats, (1, 0, 2)).reshape(half, planes, height, across)
-    return grad_feats, layout(out_one), layout(out_two)
+        return jnp.transpose(total.reshape(taps, half, total.shape[1]), (2, 1, 0))
+
+    return out_feats, layout(out_one), layout(out_two)
 
 
 def solution(mesh):

time: 45 us -> 38.4 us (0.85)
  local copies, waits for them, and re-layouts: 9.9 us -> 3.84 us
    reshape x7 -> x0, local copies, waits for them, and re-layouts: 3.81 us -> none  [the longest x2 1.53 us: forward(): jnp.transpose(weight.reshape(o, 2, half, 27), (1, 0, 3, 2))]
    unnamed x15 -> x5, local copies, waits for them, and re-layouts: 1.21 us -> 3.84 us
    slice x2 -> x0, local copies, waits for them, and re-layouts: 2.51 us -> none  [layout(): total[:, :27 * half].reshape(rows, 27, half)]
    transpose x5 -> x0, local copies, waits for them, and re-layouts: 1.51 us -> none  [the longest x4 1.5 us: backward(): jnp.transpose(weight[:, :, ::-1], (1, 2, 0)).reshape(weight.shape[1], -1)]
    another operation x1 -> x0, local copies, waits for them, and re-layouts: 0.86 us -> none  [shards(): w1b = backward(weight_one).reshape(2, half, 27 * mids)]
where the time goes in v2:
time: 38.4 us; the launch traced here: 38.2 us
  Pallas kernels  33.7 us (88%)
  local copies, waits for them, and re-layouts  3.84 us (10%)
  between operations  0.64 us (2%)
    pallas_call x1, Pallas kernels, shards(): pl.pallas_call(functools.partial(kernel, n, owners, across), out_shape=(j...  33.7 us
    unnamed x5, local copies, waits for them, and re-layouts  3.84 us

profile of v2, /device:TPU:0, one launch (start us, length us, event | category | flops | bytes accessed | tf_op | source)
XLA Modules:
  0.0 38.2 jit_solution(11697924024182126011)
XLA Ops:
  0.6 33.7 %shard_map.67 = (bf16[16,2,8,128]{3,2,1,0:T(8,128)(2,1)}, f32[432,32]{1,0:T(8,128)}, f32[432,64]{1,0:T(8,128)}) custom-call(bf16[16,2,8,128]{3,2,1,0:T(8,128)(2,1)} %feats_in.1, bf16[32,1,4,64]{3,2,1,0:T(4,128)(2,1)} %cot_in.1, bf16[27,32,32]{2,1,0:T(8,128)(2,1)} %bitcast.10, bf16[27,32,64]{2,1,0:T(8,128)(2,1)} %bitcast.11), custom_call_target="tpu_custom_call" | custom-call | tf_op jit(solution)/shard_map/pallas_call | solution.py:380
  34.4 1.5 %copy.10 = bf16[16,2,8,128]{3,2,1,0:T(8,128)(2,1)} copy(bf16[16,2,8,128]{3,2,1,0:T(8,128)(2,1)} %get-tuple-element.12) | data formatting | bytes 131072
  35.8 0.0 copy-start
  35.8 1.7 %copy.11 = f32[32,16,27]{0,1,2:T(8,128)} copy(f32[32,16,27]{0,1,2:T(8,128)} %bitcast.9) | data formatting | bytes 110592
  37.5 0.0 copy-done
  37.5 0.7 %copy.12 = f32[64,16,27]{0,1,2:T(8,128)} copy(f32[64,16,27]{0,1,2:T(8,128)S(1)} %bitcast.8) | data formatting | bytes 221184
Async XLA Ops:
  35.8 1.7 %copy-start = (f32[432,64]{1,0:T(8,128)S(1)}, f32[432,64]{1,0:T(8,128)}, u32[]{:S(2)}) copy-start(f32[432,64]{1,0:T(8,128)} %get-tuple-element.8) | copy-start | bytes 331780

commit v3 on v2

--- a/solution.py
+++ b/solution.py
@@ -52,9 +52,9 @@
     n, owners, across,
     feats_in, cot_in, w1, w2,
     out_feats, out_one, out_two,
-    feats, rel, cot, crel, w1f, w1b, w2f, w2b, halo, cots, pools, x1, x2, xg1, xg2, slopes, shrink, spread,
+    feats, rel, cot, crel, w1f, w1b, w2f, w2b, halo, cots, pools, x1, x2, xg1, xg2, slopes, edges, beyond, shrink, spread,
     part1, land1, full1, part2, land2, full2,
-    send_f, recv_f, send_c, recv_c, send_p, recv_p,
+    send_f, recv_f, send_c, recv_c, send_p, recv_p, send_e, recv_e,
     send_r1, recv_r1, send_a1, recv_a1, send_r2, recv_r2, send_a2, recv_a2,
 ):
     place = lax.axis_index("depth")
@@ -101,13 +101,14 @@
     spread[...] = jnp.where(target == small_row, 0.125, 0.0).astype(BF16)
 
     rows = cells // across
+    x1[:, 4 * rows1 :, :] = jnp.zeros((2, x1.shape[1] - 4 * rows1, cells), BF16)
     for plane in range(2):
         rel[plane] = feats_in[:, plane].astype(F32).reshape(half * rows, across)
         for row in range(rows):
             feats[plane, :, row * across : (row + 1) * across] = rel[
                 plane, pl.ds(row, half, stride=rows), :
             ].astype(BF16)
-        put_x1(2 + plane, core, feats[plane])
+        put_x1(1 + plane, core, feats[plane])
     short = small // (across // 2)
     for chan in range(cot.shape[0]):
         crel[chan * 8 : chan * 8 + short, :] = cot_in[chan, 0].astype(F32)
@@ -145,21 +146,19 @@
         for one, step in pairs:
             pl.when(valid(step))(lambda one=one: one.wait_send())
 
-    near, far = [], []
-    mate = copy(feats, halo.at[pl.ds(2, 2), core], send_f.at[0], recv_f.at[0], (place, other))
+    near = []
+    mate = copy(feats, halo.at[pl.ds(1, 2), core], send_f.at[0], recv_f.at[0], (place, other))
     mate.start()
     index = 1
-    for planes in ((1, 0), (0, 1)):
-        for step, plane in zip((1, -1), planes):
-            for who in (core, other):
-                to = plane if step == 1 else 4 + plane
-                one = copy(
-                    feats.at[plane], halo.at[to, core], send_f.at[index], recv_f.at[index],
-                    (at(step), who),
-                )
-                launch(one, step)
-                (near if index < 5 else far).append((one, step))
-                index += 1
+    for step, plane, to in ((1, 1, 0), (-1, 0, 3)):
+        for who in (core, other):
+            one = copy(
+                feats.at[plane], halo.at[to, core], send_f.at[index], recv_f.at[index],
+                (at(step), who),
+            )
+            launch(one, step)
+            near.append((one, step))
+            index += 1
     cot_copies = []
     index = 0
     targets = [(0, other)] + [(s, w) for s in (1, -1, 2, -2) for w in (core, other)]
@@ -182,18 +181,20 @@
         return total + dot(w1f[1], x1[1, (plane - 1) * rows1 : (plane + 2) * rows1, :])
 
     mate.wait_recv()
-    for plane in (2, 3):
+    for plane in (1, 2):
         take_halo(plane, other, None)
     arrive(near)
-    for plane, step in ((1, -1), (4, 1)):
+    for plane, step in ((0, -1), (3, 1)):
         for side in range(2):
             take_halo(plane, side, valid(step))
 
     pooled = None
-    for plane in (2, 3):
-        pre = conv_one(plane)
+    for plane in range(2):
+        pre = conv_one(plane + 1)
         sig = jax.nn.sigmoid(pre)
-        slopes[plane - 1] = sig * (1.0 + pre * (1.0 - sig))
+        bend = sig * (1.0 + pre * (1.0 - sig))
+        slopes[plane] = bend
+        edges[plane] = bend.astype(BF16)
         term = dot((pre * sig).astype(BF16), shrink[...])
         pooled = term if pooled is None else pooled + term
     pools[3] = pooled.astype(BF16)
@@ -205,12 +206,14 @@
         launch(one, step)
         pool_copies.append((one, step))
 
-    arrive(far)
-    for plane, step in ((0, -1), (5, 1)):
-        for side in range(2):
-            take_halo(plane, side, valid(step))
-    for plane in (1, 4):
-        slopes[plane - 1] = slope(conv_one(plane))
+    edge_copies = []
+    for index, step in enumerate((1, -1)):
+        one = copy(
+            edges.at[1 - index], beyond.at[index], send_e.at[index], recv_e.at[index],
+            (at(step), core),
+        )
+        launch(one, step)
+        edge_copies.append((one, step))
 
     def put_x2(plane, keep):
         field = pools[plane].astype(F32)
@@ -222,25 +225,23 @@
                     side * half : (side + 1) * half
                 ]
 
-    put_x2(3, None)
-    arrive(cot_copies)
-    arrive(pool_copies)
-    for plane in (2, 4, 1, 5, 0, 6):
-        put_x2(plane, valid(plane - 3))
-
     rows2 = 9 * outs
-    own_grad = None
-    for plane in range(5):
+
+    def level_two(plane):
         pre = dot(w2f[0], x2[0, plane * rows1 : (plane + 3) * rows1, :])
         pre = pre + dot(w2f[1], x2[1, plane * rows1 : (plane + 3) * rows1, :])
         grad = cots[plane].reshape(outs, small).astype(F32) * slope(pre)
         if plane != 2:
             grad = jnp.where(valid(plane - 2), grad, 0.0)
-        else:
-            own_grad = grad.astype(BF16)
-        grad = grad.astype(BF16)
+        return grad.astype(BF16)
+
+    def put_xg2(plane, grad):
         for tap, block in enumerate(plane_taps(grad, across // 2)):
             xg2[pl.ds((4 - plane) * rows2 + (8 - tap) * outs, outs), :] = block
+
+    def back(plane):
+        total = dot(w2b[...], xg2[(2 - plane) * rows2 : (5 - plane) * rows2, :])
+        return dot(total.astype(BF16), spread[...])
 
     lanes = 512
     mine = place // stride
@@ -325,24 +326,43 @@
         ]
         out[...] = jnp.concatenate(bands, axis=0).T[: out.shape[0]]
 
-    total2 = dot_nt(own_grad, x2[core, 2 * rows1 : 2 * rows1 + lanes, :])
+    put_x2(3, None)
+    arrive(cot_copies[:1])
+    arrive(pool_copies[:2])
+    for plane in (2, 4):
+        put_x2(plane, valid(plane - 3))
+    grad = level_two(2)
+    total2 = dot_nt(grad, x2[core, 2 * rows1 : 2 * rows1 + lanes, :])
     chunk_out(total2, part2)
     scatter(part2, land2, send_r2, recv_r2)
-
-    grads = []
-    for plane in range(3):
-        back = dot(w2b[...], xg2[(2 - plane) * rows2 : (5 - plane) * rows2, :]).astype(BF16)
-        wide = dot(back, spread[...])
-        for where in ((0,), (1, 2), (3,))[plane]:
-            grad = wide * slopes[where]
-            if plane != 1:
-                grad = jnp.where(valid(plane - 1), grad, 0.0)
-            grads.append(grad.astype(BF16))
-
-    total1 = dot_nt(grads[1], x1[core, rows1 : rows1 + lanes, :])
-    total1 = total1 + dot_nt(grads[2], x1[core, 2 * rows1 : 2 * rows1 + lanes, :])
+    put_xg2(2, grad)
+
+    arrive(cot_copies[1:5])
+    arrive(pool_copies[2:4])
+    for plane in (1, 5):
+        put_x2(plane, valid(plane - 3))
+    for plane in (1, 3):
+        put_xg2(plane, level_two(plane))
+
+    wide = back(1)
+    inner = [(wide * slopes[plane]).astype(BF16) for plane in range(2)]
+    total1 = dot_nt(inner[0], x1[core, :lanes, :])
+    total1 = total1 + dot_nt(inner[1], x1[core, rows1 : rows1 + lanes, :])
     chunk_out(total1, part1)
     scatter(part1, land1, send_r1, recv_r1)
+
+    arrive(cot_copies[5:])
+    arrive(pool_copies[4:])
+    for plane in (0, 6):
+        put_x2(plane, valid(plane - 3))
+    for plane in (0, 4):
+        put_xg2(plane, level_two(plane))
+    arrive(edge_copies)
+    outer = []
+    for index, step in enumerate((-1, 1)):
+        grad = back(1 + step) * beyond[index].astype(F32)
+        outer.append(jnp.where(valid(step), grad, 0.0).astype(BF16))
+    grads = [outer[0], inner[0], inner[1], outer[1]]
     gather(part2, land2, full2, recv_r2, send_a2, recv_a2)
 
     rows_g = 9 * mids
@@ -359,7 +379,7 @@
 
     gather(part1, land1, full1, recv_r1, send_a1, recv_a1)
     mate.wait_send()
-    leave(near + far + cot_copies + pool_copies)
+    leave(near + cot_copies + pool_copies + edge_copies)
     finish(part2, land2, full2, send_r2, send_a2, recv_a2, out_two)
     finish(part1, land1, full1, send_r1, send_a1, recv_a1, out_one)
 
@@ -395,14 +415,16 @@
             pltpu.VMEM((2, half, taps * mids), BF16),
             pltpu.VMEM((2, outs, taps * half), BF16),
             pltpu.VMEM((mids, taps * outs), BF16),
-            pltpu.VMEM((6, 2, half, cells), BF16),
+            pltpu.VMEM((4, 2, half, cells), BF16),
             pltpu.VMEM((5, 2, outs // 2, small), BF16),
             pltpu.VMEM((7, mids, small), BF16),
-            pltpu.VMEM((2, 6 * 9 * half, cells), BF16),
+            pltpu.VMEM((2, 5 * 9 * half, cells), BF16),
             pltpu.VMEM((2, 7 * 9 * half, small), BF16),
             pltpu.VMEM((4 * 9 * mids, cells), BF16),
             pltpu.VMEM((5 * 9 * outs, small), BF16),
-            pltpu.VMEM((4, mids, cells), F32),
+            pltpu.VMEM((2, mids, cells), F32),
+            pltpu.VMEM((2, mids, cells), BF16),
+            pltpu.VMEM((2, mids, cells), BF16),
             pltpu.VMEM((cells, small), BF16),
             pltpu.VMEM((small, cells), BF16),
             pltpu.VMEM((owners, mids // 4, 128), BF16),
@@ -411,7 +433,7 @@
             pltpu.VMEM((owners, outs // 4, 128), BF16),
             pltpu.VMEM((n, outs // 4, 128), BF16),
             pltpu.VMEM((owners, outs // 4, 128), BF16),
-            dma((9,)), dma((9,)), dma((9,)), dma((9,)), dma((6,)), dma((6,)),
+            dma((5,)), dma((5,)), dma((9,)), dma((9,)), dma((6,)), dma((6,)), dma((2,)), dma((2,)),
             dma((owners,)), dma((n,)), dma((n,)), dma((owners,)),
             dma((owners,)), dma((n,)), dma((n,)), dma((owners,)),
         ],

time: 38.4 us -> 36.7 us (0.956)
  Pallas kernels: 33.7 us -> 32 us
    pallas_call x1, Pallas kernels: 33.7 us -> 32 us  [shards(): pl.pallas_call(functools.partial(kernel, n, owners, across), out_shape=(j...]
where the time goes in v3:
time: 36.7 us; the launch traced here: 36.5 us
  Pallas kernels  32 us (87%)
  local copies, waits for them, and re-layouts  3.84 us (10%)
  between operations  0.64 us (2%)
    pallas_call x1, Pallas kernels, shards(): pl.pallas_call(functools.partial(kernel, n, owners, across), out_shape=(j...  32 us
    unnamed x5, local copies, waits for them, and re-layouts  3.84 us

profile of v3, /device:TPU:0, one launch (start us, length us, event | category | flops | bytes accessed | tf_op | source)
XLA Modules:
  0.0 36.5 jit_solution(15556767323661371320)
XLA Ops:
  0.6 32.0 %shard_map.67 = (bf16[16,2,8,128]{3,2,1,0:T(8,128)(2,1)}, f32[432,32]{1,0:T(8,128)}, f32[432,64]{1,0:T(8,128)}) custom-call(bf16[16,2,8,128]{3,2,1,0:T(8,128)(2,1)} %feats_in.1, bf16[32,1,4,64]{3,2,1,0:T(4,128)(2,1)} %cot_in.1, bf16[27,32,32]{2,1,0:T(8,128)(2,1)} %bitcast.10, bf16[27,32,64]{2,1,0:T(8,128)(2,1)} %bitcast.11), custom_call_target="tpu_custom_call" | custom-call | tf_op jit(solution)/shard_map/pallas_call | solution.py:400
  32.7 1.5 %copy.10 = bf16[16,2,8,128]{3,2,1,0:T(8,128)(2,1)} copy(bf16[16,2,8,128]{3,2,1,0:T(8,128)(2,1)} %get-tuple-element.12) | data formatting | bytes 131072
  34.1 0.0 copy-start
  34.1 1.7 %copy.11 = f32[32,16,27]{0,1,2:T(8,128)} copy(f32[32,16,27]{0,1,2:T(8,128)} %bitcast.9) | data formatting | bytes 110592
  35.8 0.0 copy-done
  35.8 0.7 %copy.12 = f32[64,16,27]{0,1,2:T(8,128)} copy(f32[64,16,27]{0,1,2:T(8,128)S(1)} %bitcast.8) | data formatting | bytes 221184
Async XLA Ops:
  34.1 1.7 %copy-start = (f32[432,64]{1,0:T(8,128)S(1)}, f32[432,64]{1,0:T(8,128)}, u32[]{:S(2)}) copy-start(f32[432,64]{1,0:T(8,128)} %get-tuple-element.8) | copy-start | bytes 331780

commit v4 on v3

--- a/solution.py
+++ b/solution.py
@@ -50,11 +50,11 @@
 
 def kernel(
     n, owners, across,
-    feats_in, cot_in, w1, w2,
+    feats_hbm, cot_hbm, w1_hbm, w2_hbm,
     out_feats, out_one, out_two,
-    feats, rel, cot, crel, w1f, w1b, w2f, w2b, halo, cots, pools, x1, x2, xg1, xg2, slopes, edges, beyond, shrink, spread,
+    feats_in, cot_in, w1, w2, feats, rel, cot, crel, w1f, w1b, w2f, w2b, halo, cots, pools, x1, x2, xg1, xg2, slopes, edges, beyond, shrink, spread,
     part1, land1, full1, part2, land2, full2,
-    send_f, recv_f, send_c, recv_c, send_p, recv_p, send_e, recv_e,
+    send_f, recv_f, send_c, recv_c, load, send_p, recv_p, send_e, recv_e,
     send_r1, recv_r1, send_a1, recv_a1, send_r2, recv_r2, send_a2, recv_a2,
 ):
     place = lax.axis_index("depth")
@@ -84,6 +84,15 @@
 
     lax.fori_loop(1, n, greet_row, 0)
 
+    loads = [
+        pltpu.make_async_copy(source, target, load.at[index])
+        for index, (source, target) in enumerate(
+            ((feats_hbm, feats_in), (cot_hbm, cot_in), (w1_hbm, w1), (w2_hbm, w2))
+        )
+    ]
+    for one in loads:
+        one.start()
+
     def valid(step):
         return jnp.logical_and(place + step >= 0, place + step < n)
 
@@ -91,42 +100,20 @@
         for tap, block in enumerate(plane_taps(field, across)):
             x1[side, pl.ds(plane * rows1 + tap * half, half), :] = block
 
-    big_row = lax.broadcasted_iota(jnp.int32, (cells, small), 0)
-    small_col = lax.broadcasted_iota(jnp.int32, (cells, small), 1)
-    target = (big_row // (2 * across)) * (across // 2) + lax.rem(big_row, across) // 2
-    shrink[...] = jnp.where(target == small_col, 0.125, 0.0).astype(BF16)
-    big_col = lax.broadcasted_iota(jnp.int32, (small, cells), 1)
-    small_row = lax.broadcasted_iota(jnp.int32, (small, cells), 0)
-    target = (big_col // (2 * across)) * (across // 2) + lax.rem(big_col, across) // 2
-    spread[...] = jnp.where(target == small_row, 0.125, 0.0).astype(BF16)
-
     rows = cells // across
-    x1[:, 4 * rows1 :, :] = jnp.zeros((2, x1.shape[1] - 4 * rows1, cells), BF16)
+    loads[0].wait()
     for plane in range(2):
         rel[plane] = feats_in[:, plane].astype(F32).reshape(half * rows, across)
         for row in range(rows):
             feats[plane, :, row * across : (row + 1) * across] = rel[
                 plane, pl.ds(row, half, stride=rows), :
             ].astype(BF16)
-        put_x1(1 + plane, core, feats[plane])
+    loads[1].wait()
     short = small // (across // 2)
     for chan in range(cot.shape[0]):
         crel[chan * 8 : chan * 8 + short, :] = cot_in[chan, 0].astype(F32)
     lines = [crel[pl.ds(row, cot.shape[0], stride=8), :] for row in range(short)]
     cot[...] = jnp.concatenate(lines, axis=1).astype(BF16)
-    cots[2, core] = cot[...]
-
-    taps, mids, _ = w1.shape
-    outs = w2.shape[2]
-    for side in range(2):
-        lo, hi = side * half, (side + 1) * half
-        for tap in range(taps):
-            w1f[side, :, tap * half : (tap + 1) * half] = w1[tap][:, lo:hi]
-        w2f[side] = w2[:, lo:hi, :].reshape(taps * half, outs).T
-    w1b[...] = w1[...].reshape(taps * mids, mids).T.reshape(2, half, taps * mids)
-    for tap in range(taps):
-        w2b[:, tap * outs : (tap + 1) * outs] = w2[tap]
-
     pl.semaphore_wait(barrier, n + 4)
 
     def copy(src, dst, send, recv, device):
@@ -180,6 +167,32 @@
         total = dot(w1f[0], x1[0, (plane - 1) * rows1 : (plane + 2) * rows1, :])
         return total + dot(w1f[1], x1[1, (plane - 1) * rows1 : (plane + 2) * rows1, :])
 
+    cots[2, core] = cot[...]
+
+    for plane in range(2):
+        put_x1(1 + plane, core, feats[plane])
+    x1[:, 4 * rows1 :, :] = jnp.zeros((2, x1.shape[1] - 4 * rows1, cells), BF16)
+    loads[2].wait()
+    loads[3].wait()
+    taps, mids, _ = w1.shape
+    outs = w2.shape[2]
+    for side in range(2):
+        lo, hi = side * half, (side + 1) * half
+        for tap in range(taps):
+            w1f[side, :, tap * half : (tap + 1) * half] = w1[tap][:, lo:hi]
+        w2f[side] = w2[:, lo:hi, :].reshape(taps * half, outs).T
+    w1b[...] = w1[...].reshape(taps * mids, mids).T.reshape(2, half, taps * mids)
+    for tap in range(taps):
+        w2b[:, tap * outs : (tap + 1) * outs] = w2[tap]
+    big_row = lax.broadcasted_iota(jnp.int32, (cells, small), 0)
+    small_col = lax.broadcasted_iota(jnp.int32, (cells, small), 1)
+    target = (big_row // (2 * across)) * (across // 2) + lax.rem(big_row, across) // 2
+    shrink[...] = jnp.where(target == small_col, 0.125, 0.0).astype(BF16)
+    big_col = lax.broadcasted_iota(jnp.int32, (small, cells), 1)
+    small_row = lax.broadcasted_iota(jnp.int32, (small, cells), 0)
+    target = (big_col // (2 * across)) * (across // 2) + lax.rem(big_col, across) // 2
+    spread[...] = jnp.where(target == small_row, 0.125, 0.0).astype(BF16)
+
     mate.wait_recv()
     for plane in (1, 2):
         take_halo(plane, other, None)
@@ -404,9 +417,13 @@
             jax.ShapeDtypeStruct((taps * half, mids), F32),
             jax.ShapeDtypeStruct((taps * half, outs), F32),
         ),
-        in_specs=[vmem] * 4,
+        in_specs=[pl.BlockSpec(memory_space=pl.ANY)] * 4,
         out_specs=(vmem,) * 3,
         scratch_shapes=[
+            pltpu.VMEM(feats.shape, BF16),
+            pltpu.VMEM(cotangent.shape, BF16),
+            pltpu.VMEM(w1.shape, BF16),
+            pltpu.VMEM(w2.shape, BF16),
             pltpu.VMEM((planes, half, cells), BF16),
             pltpu.VMEM((planes, half * height, across), F32),
             pltpu.VMEM((outs // 2, small), BF16),
@@ -433,7 +450,7 @@
             pltpu.VMEM((owners, outs // 4, 128), BF16),
             pltpu.VMEM((n, outs // 4, 128), BF16),
             pltpu.VMEM((owners, outs // 4, 128), BF16),
-            dma((5,)), dma((5,)), dma((9,)), dma((9,)), dma((6,)), dma((6,)), dma((2,)), dma((2,)),
+            dma((5,)), dma((5,)), dma((9,)), dma((9,)), dma((4,)), dma((6,)), dma((6,)), dma((2,)), dma((2,)),
             dma((owners,)), dma((n,)), dma((n,)), dma((owners,)),
             dma((owners,)), dma((n,)), dma((n,)), dma((owners,)),
         ],

time: 36.7 us -> 35.9 us (0.978)
  Pallas kernels: 32 us -> 31.2 us
    pallas_call x1, Pallas kernels: 32 us -> 31.2 us  [shards(): pl.pallas_call(functools.partial(kernel, n, owners, across), out_shape=(j...]
where the time goes in v4:
time: 35.9 us; the launch traced here: 35.7 us
  Pallas kernels  31.2 us (87%)
  local copies, waits for them, and re-layouts  3.84 us (11%)
  between operations  0.64 us (2%)
    pallas_call x1, Pallas kernels, shards(): pl.pallas_call(functools.partial(kernel, n, owners, across), out_shape=(j...  31.2 us
    unnamed x5, local copies, waits for them, and re-layouts  3.84 us

profile of v4, /device:TPU:0, one launch (start us, length us, event | category | flops | bytes accessed | tf_op | source)
XLA Modules:
  0.0 35.7 jit_solution(11450752274034232158)
XLA Ops:
  0.6 31.2 %shard_map.67 = (bf16[16,2,8,128]{3,2,1,0:T(8,128)(2,1)}, f32[432,32]{1,0:T(8,128)}, f32[432,64]{1,0:T(8,128)}) custom-call(bf16[16,2,8,128]{3,2,1,0:T(8,128)(2,1)} %feats_hbm.1, bf16[32,1,4,64]{3,2,1,0:T(4,128)(2,1)} %cot_hbm.1, bf16[27,32,32]{2,1,0:T(8,128)(2,1)} %bitcast.10, bf16[27,32,64]{2,1,0:T(8,128)(2,1)} %bitcast.11), custom_call_target="tpu_custom_call" | custom-call | tf_op jit(solution)/shard_map/pallas_call | solution.py:413
  31.8 1.5 %copy.10 = bf16[16,2,8,128]{3,2,1,0:T(8,128)(2,1)} copy(bf16[16,2,8,128]{3,2,1,0:T(8,128)(2,1)} %get-tuple-element.12) | data formatting | bytes 131072
  33.3 0.0 copy-start
  33.3 1.7 %copy.11 = f32[32,16,27]{0,1,2:T(8,128)} copy(f32[32,16,27]{0,1,2:T(8,128)} %bitcast.9) | data formatting | bytes 110592
  35.0 0.0 copy-done
  35.0 0.7 %copy.12 = f32[64,16,27]{0,1,2:T(8,128)} copy(f32[64,16,27]{0,1,2:T(8,128)S(1)} %bitcast.8) | data formatting | bytes 221184
Async XLA Ops:
  33.3 1.7 %copy-start = (f32[432,64]{1,0:T(8,128)S(1)}, f32[432,64]{1,0:T(8,128)}, u32[]{:S(2)}) copy-start(f32[432,64]{1,0:T(8,128)} %get-tuple-element.8) | copy-start | bytes 331780

commit v5 on v4

--- a/solution.py
+++ b/solution.py
@@ -333,11 +333,7 @@
 
             lax.fori_loop(1, n, sent, 0)
 
-        bands = [
-            jnp.concatenate([full[4 * r + l].astype(F32) for l in range(4)], axis=1)
-            for r in range(owners // 4)
-        ]
-        out[...] = jnp.concatenate(bands, axis=0).T[: out.shape[0]]
+        out[...] = full[...]
 
     put_x2(3, None)
     arrive(cot_copies[:1])
@@ -384,17 +380,29 @@
             xg1[pl.ds((3 - plane) * rows_g + (8 - tap) * mids, mids), :] = block
     for plane in range(2):
         field = dot(w1b[core], xg1[(1 - plane) * rows_g : (4 - plane) * rows_g, :])
-        for row in range(rows):
-            rel[plane, pl.ds(row, half, stride=rows), :] = field[
-                :, row * across : (row + 1) * across
-            ]
-        out_feats[:, plane] = rel[plane].reshape(half, rows, across).astype(BF16)
+        out_feats[plane] = field.astype(BF16)
 
     gather(part1, land1, full1, recv_r1, send_a1, recv_a1)
     mate.wait_send()
     leave(near + cot_copies + pool_copies + edge_copies)
     finish(part2, land2, full2, send_r2, send_a2, recv_a2, out_two)
     finish(part1, land1, full1, send_r1, send_a1, recv_a1, out_one)
+
+
+def layout_kernel(fields, one, two, out_feats, out_one, out_two, rel):
+    half, planes, rows, across = out_feats.shape
+    for plane in range(planes):
+        for row in range(rows):
+            rel[plane, pl.ds(row, half, stride=rows), :] = fields[
+                plane, :, row * across : (row + 1) * across
+            ].astype(F32)
+        out_feats[:, plane] = rel[plane].reshape(half, rows, across).astype(BF16)
+    for full, out in ((one, out_one), (two, out_two)):
+        bands = [
+            jnp.concatenate([full[4 * r + l].astype(F32) for l in range(4)], axis=1)
+            for r in range(full.shape[0] // 4)
+        ]
+        out[...] = jnp.concatenate(bands, axis=0).T[: out.shape[0]]
 
 
 def shards(feats, weight_one, weight_two, cotangent):
@@ -410,14 +418,14 @@
     w2 = jnp.transpose(weight_two, (2, 1, 0))
     vmem = pl.BlockSpec(memory_space=pltpu.VMEM)
     dma = pltpu.SemaphoreType.DMA
-    out_feats, out_one, out_two = pl.pallas_call(
+    packed = pl.pallas_call(
         functools.partial(kernel, n, owners, across),
         out_shape=(
-            jax.ShapeDtypeStruct(feats.shape, BF16),
-            jax.ShapeDtypeStruct((taps * half, mids), F32),
-            jax.ShapeDtypeStruct((taps * half, outs), F32),
+            jax.ShapeDtypeStruct((planes, half, cells), BF16),
+            jax.ShapeDtypeStruct((owners, mids // 4, 128), BF16),
+            jax.ShapeDtypeStruct((owners, outs // 4, 128), BF16),
         ),
-        in_specs=[pl.BlockSpec(memory_space=pl.ANY)] * 4,
+        in_specs=[pl.BlockSpec(memory_space=pltpu.HBM)] * 4,
         out_specs=(vmem,) * 3,
         scratch_shapes=[
             pltpu.VMEM(feats.shape, BF16),
@@ -455,9 +463,22 @@
             dma((owners,)), dma((n,)), dma((n,)), dma((owners,)),
         ],
         compiler_params=pltpu.CompilerParams(
-            collective_id=0, has_side_effects=True, vmem_limit_bytes=60 * 1024 * 1024
+            collective_id=0, has_side_effects=True, vmem_limit_bytes=28 * 1024 * 1024
         ),
     )(feats, cotangent, w1, w2)
+
+    out_feats, out_one, out_two = pl.pallas_call(
+        layout_kernel,
+        out_shape=(
+            jax.ShapeDtypeStruct(feats.shape, BF16),
+            jax.ShapeDtypeStruct((taps * half, mids), F32),
+            jax.ShapeDtypeStruct((taps * half, outs), F32),
+        ),
+        in_specs=[vmem] * 3,
+        out_specs=(vmem,) * 3,
+        scratch_shapes=[pltpu.VMEM((planes, half * height, across), F32)],
+        compiler_params=pltpu.CompilerParams(vmem_limit_bytes=8 * 1024 * 1024),
+    )(*packed)
 
     def layout(total):
         return jnp.transpose(total.reshape(taps, half, total.shape[1]), (2, 1, 0))

time: 35.9 us -> 35.4 us (0.986)
  local copies, waits for them, and re-layouts: 3.84 us -> 3.46 us
    pallas_call x1, Pallas kernels: 31.2 us -> 30.1 us  [shards(): pl.pallas_call(functools.partial(kernel, n, owners, across), out_shape=(j...]
    pallas_call x0 -> x1, Pallas kernels: none -> 0.88 us  [shards(): pl.pallas_call(layout_kernel, out_shape=(jax.ShapeDtypeStruct(feats.shape...]
    unnamed x5 -> x8, local copies, waits for them, and re-layouts: 3.84 us -> 3.46 us
where the time goes in v5:
time: 35.4 us; the launch traced here: 35.1 us
  Pallas kernels  31 us (88%)
  local copies, waits for them, and re-layouts  3.46 us (10%)
  between operations  0.65 us (2%)
    pallas_call x1, Pallas kernels, shards(): pl.pallas_call(functools.partial(kernel, n, owners, across), out_shape=(j...  30.1 us
    unnamed x8, local copies, waits for them, and re-layouts  3.46 us
    pallas_call x1, Pallas kernels, shards(): pl.pallas_call(layout_kernel, out_shape=(jax.ShapeDtypeStruct(feats.shape...  0.88 us

profile of v5, /device:TPU:0, one launch (start us, length us, event | category | flops | bytes accessed | tf_op | source)
XLA Modules:
  0.0 35.1 jit_solution(1833382453051521469)
XLA Ops:
  0.6 0.0 copy-start
  0.6 0.9 %copy-done = bf16[32,32,27]{1,0,2:T(8,128)(2,1)S(1)} copy-done((bf16[32,32,27]{1,0,2:T(8,128)(2,1)S(1)}, bf16[32,32,27]{1,0,2:T(8,128)(2,1)}, u32[]{:S(2)}) %copy-start) | copy-done | bytes 55320
  1.6 0.0 copy-start.1
  1.6 0.9 %copy-done.1 = bf16[64,32,27]{0,1,2:T(8,128)(2,1)S(1)} copy-done((bf16[64,32,27]{0,1,2:T(8,128)(2,1)S(1)}, bf16[64,32,27]{0,1,2:T(8,128)(2,1)}, u32[]{:S(2)}) %copy-start.1) | copy-done | bytes 110616
  2.5 0.0 copy-start.2
  2.5 0.8 %copy-done.2 = bf16[16,2,8,128]{3,2,1,0:T(8,128)(2,1)S(1)} copy-done((bf16[16,2,8,128]{3,2,1,0:T(8,128)(2,1)S(1)}, bf16[16,2,8,128]{3,2,1,0:T(8,128)(2,1)}, u32[]{:S(2)}) %copy-start.2) | copy-done | bytes 65560
  3.3 0.0 copy-start.3
  3.3 0.8 %copy-done.3 = bf16[32,1,4,64]{3,2,1,0:T(4,128)(2,1)S(1)} copy-done((bf16[32,1,4,64]{3,2,1,0:T(4,128)(2,1)S(1)}, bf16[32,1,4,64]{3,2,1,0:T(4,128)(2,1)}, u32[]{:S(2)}) %copy-start.3) | copy-done | bytes 16408
  4.1 30.1 %shard_map.67 = (bf16[2,16,1024]{2,1,0:T(8,128)(2,1)S(1)}, bf16[16,8,128]{2,1,0:T(8,128)(2,1)S(1)}, bf16[16,16,128]{2,1,0:T(8,128)(2,1)S(1)}) custom-call(bf16[16,2,8,128]{3,2,1,0:T(8,128)(2,1)S(1)} %copy-done.2, bf16[32,1,4,64]{3,2,1,0:T(4,128)(2,1)S(1)} %copy-done.3, bf16[27,32,32]{2,1,0:T(8,128)(2,1)S(1)} %bitcast.8, bf16[27,32,64]{2,1,0:T(8,128)(2,1)S(1)} %bitcast.9), custom_call_target="tpu_custom_call" | custom-call | tf_op jit(solution)/shard_map/pallas_call | solution.py:421
  34.2 0.9 %shard_map.68 = (bf16[16,2,8,128]{3,2,1,0:T(8,128)(2,1)}, f32[432,32]{1,0:T(8,128)}, f32[432,64]{1,0:T(8,128)}) custom-call(bf16[2,16,1024]{2,1,0:T(8,128)(2,1)S(1)} %get-tuple-element.9.fields, bf16[16,8,128]{2,1,0:T(8,128)(2,1)S(1)} %get-tuple-element.10.one, bf16[16,16,128]{2,1,0:T(8,128)(2,1)S(1)} %get-tuple-element.11.two), custom_call_target="tpu_custom_call" | custom-call | tf_op jit(solution)/shard_map/pallas_call | solution.py:470
Async XLA Ops:
  0.6 0.9 %copy-start = (bf16[32,32,27]{1,0,2:T(8,128)(2,1)S(1)}, bf16[32,32,27]{1,0,2:T(8,128)(2,1)}, u32[]{:S(2)}) copy-start(bf16[32,32,27]{1,0,2:T(8,128)(2,1)} %param.5) | copy-start | bytes 165892
  1.6 0.9 %copy-start.1 = (bf16[64,32,27]{0,1,2:T(8,128)(2,1)S(1)}, bf16[64,32,27]{0,1,2:T(8,128)(2,1)}, u32[]{:S(2)}) copy-start(bf16[64,32,27]{0,1,2:T(8,128)(2,1)} %param.6) | copy-start | bytes 331780
  2.5 0.8 %copy-start.2 = (bf16[16,2,8,128]{3,2,1,0:T(8,128)(2,1)S(1)}, bf16[16,2,8,128]{3,2,1,0:T(8,128)(2,1)}, u32[]{:S(2)}) copy-start(bf16[16,2,8,128]{3,2,1,0:T(8,128)(2,1)} %feats_hbm.1) | copy-start | bytes 196612
  3.3 0.8 %copy-start.3 = (bf16[32,1,4,64]{3,2,1,0:T(4,128)(2,1)S(1)}, bf16[32,1,4,64]{3,2,1,0:T(4,128)(2,1)}, u32[]{:S(2)}) copy-start(bf16[32,1,4,64]{3,2,1,0:T(4,128)(2,1)} %cot_hbm.1) | copy-start | bytes 49156

commit v6 on v5

--- a/solution.py
+++ b/solution.py
@@ -425,7 +425,7 @@
             jax.ShapeDtypeStruct((owners, mids // 4, 128), BF16),
             jax.ShapeDtypeStruct((owners, outs // 4, 128), BF16),
         ),
-        in_specs=[pl.BlockSpec(memory_space=pltpu.HBM)] * 4,
+        in_specs=[pl.BlockSpec(memory_space=pl.ANY)] * 4,
         out_specs=(vmem,) * 3,
         scratch_shapes=[
             pltpu.VMEM(feats.shape, BF16),
@@ -463,7 +463,7 @@
             dma((owners,)), dma((n,)), dma((n,)), dma((owners,)),
         ],
         compiler_params=pltpu.CompilerParams(
-            collective_id=0, has_side_effects=True, vmem_limit_bytes=28 * 1024 * 1024
+            collective_id=0, has_side_effects=True, vmem_limit_bytes=60 * 1024 * 1024
         ),
     )(feats, cotangent, w1, w2)
 
@@ -477,7 +477,7 @@
         in_specs=[vmem] * 3,
         out_specs=(vmem,) * 3,
         scratch_shapes=[pltpu.VMEM((planes, half * height, across), F32)],
-        compiler_params=pltpu.CompilerParams(vmem_limit_bytes=8 * 1024 * 1024),
+        compiler_params=pltpu.CompilerParams(vmem_limit_bytes=60 * 1024 * 1024),
     )(*packed)
 
     def layout(total):

time: 35.4 us -> 33.5 us (0.946)
  local copies, waits for them, and re-layouts: 3.46 us -> 0 us
  Pallas kernels: 31 us -> 32.7 us
    unnamed x8 -> x0, local copies, waits for them, and re-layouts: 3.46 us -> none
    pallas_call x1, Pallas kernels: 0.88 us -> 1.77 us  [shards(): pl.pallas_call(layout_kernel, out_shape=(jax.ShapeDtypeStruct(feats.shape...]
    pallas_call x1, Pallas kernels: 30.1 us -> 31 us  [shards(): pl.pallas_call(functools.partial(kernel, n, owners, across), out_shape=(j...]
where the time goes in v6:
time: 33.5 us; the launch traced here: 33.4 us
  Pallas kernels  32.7 us (98%)
  between operations  0.64 us (2%)
    pallas_call x1, Pallas kernels, shards(): pl.pallas_call(functools.partial(kernel, n, owners, across), out_shape=(j...  31 us
    pallas_call x1, Pallas kernels, shards(): pl.pallas_call(layout_kernel, out_shape=(jax.ShapeDtypeStruct(feats.shape...  1.77 us

profile of v6, /device:TPU:0, one launch (start us, length us, event | category | flops | bytes accessed | tf_op | source)
XLA Modules:
  0.0 33.4 jit_solution(4578232215098679109)
XLA Ops:
  0.6 31.0 %shard_map.67 = (bf16[2,16,1024]{2,1,0:T(8,128)(2,1)}, bf16[16,8,128]{2,1,0:T(8,128)(2,1)}, bf16[16,16,128]{2,1,0:T(8,128)(2,1)}) custom-call(bf16[16,2,8,128]{3,2,1,0:T(8,128)(2,1)} %feats_hbm.1, bf16[32,1,4,64]{3,2,1,0:T(4,128)(2,1)} %cot_hbm.1, bf16[27,32,32]{2,1,0:T(8,128)(2,1)} %bitcast.8, bf16[27,32,64]{2,1,0:T(8,128)(2,1)} %bitcast.9), custom_call_target="tpu_custom_call" | custom-call | tf_op jit(solution)/shard_map/pallas_call | solution.py:421
  31.6 1.8 %shard_map.68 = (bf16[16,2,8,128]{3,2,1,0:T(8,128)(2,1)}, f32[432,32]{1,0:T(8,128)}, f32[432,64]{1,0:T(8,128)}) custom-call(bf16[2,16,1024]{2,1,0:T(8,128)(2,1)} %get-tuple-element.9.fields, bf16[16,8,128]{2,1,0:T(8,128)(2,1)} %get-tuple-element.10.one, bf16[16,16,128]{2,1,0:T(8,128)(2,1)} %get-tuple-element.11.two), custom_call_target="tpu_custom_call" | custom-call | tf_op jit(solution)/shard_map/pallas_call | solution.py:470
